TPU v7x, 128 devices: a whole 4x4x4 slice. The times are simulated.
128 devices in a mesh: teacher: 8 (over z_hi, y), student: 16 (over z_lo, x, core).
Axes of the slice: x: 4, y: 4, z: 4 (z_hi: 2, z_lo: 2; z = z_hi * 2 + z_lo), core: 2. Of those that a mesh axis runs over, the one named last changes fastest.
Arguments:
- teacher_in: bfloat16 [16384, 8192], P('student', 'teacher')
- teacher_attn: bfloat16 [16384, 4096], P('student', 'teacher'), may hold values from -6 to 6
- teacher_out_proj: bfloat16 [4096, 8192], P('student', 'teacher'), may hold values from -0.09375 to 0.09375
- teacher_gain: bfloat16 [8192], P('teacher'), may hold values from 0.099609375 to 1.8984375
- projection: bfloat16 [8192, 4096], P('teacher', 'student'), may hold values from -0.0625 to 0.0625
- student_in: bfloat16 [16384, 4096], P('student', 'teacher')
- student_attn: bfloat16 [16384, 2048], P('student', 'teacher'), may hold values from -6 to 6
- student_out_proj: bfloat16 [2048, 4096], P('student', 'teacher'), may hold values from -0.125 to 0.125
- student_gain: bfloat16 [4096], P('teacher'), may hold values from 0.099609375 to 1.8984375
- token_ids: int32 [16384], P('student'), may hold values from 0 to 128004, as said below
- row_order: int32 [16384], replicated, may hold values from 0 to 16383, as said below
Outputs:
- grad_weight: float32 [2048, 4096], P('student', 'teacher')
- grad_gain: float32 [4096], P('teacher')
Inputs may be any that keep to these rules, and one draw needn't show every extreme that they name: `token_ids`: within each sequence of 1024 consecutive rows the rows holding 128004 form the sequence's tail, after at least 256 other rows; no other row holds 128004. `row_order`: A permutation of the 16384 rows. For student block k and teacher block b (blocks of 1024 rows), the entries k * 1024 + b * 64 to k * 1024 + (b + 1) * 64 - 1 name rows of teacher block b.
All inputs are finite; a program needn't handle non-finite values.
Results may differ from a plain program's by a relative error of at most 0.02.
Values may be sent and summed in bfloat16 or wider, within the bound.
A program may use at most 128 MiB of HBM per device.

v0:
```python
import math

import jax
import jax.numpy as jnp
from jax import lax
from jax.sharding import PartitionSpec as P

DT = 8192
DS = 4096
PAD_ID = 128004


epsilon = 1e-05


def rows_first(arrays, axis, dims):
    turned = [jnp.moveaxis(a, dim, 0) for a, dim in zip(arrays, dims)]
    both = jnp.concatenate([t.reshape(len(t), -1) for t in turned], axis=1)
    result, at, outs = (lax.all_gather(both, axis, axis=0, tiled=True), 0, [])
    for t, dim in zip(turned, dims):
        section = result[:, at : at + t[0].size].reshape(-1, *t.shape[1:])
        outs.append(jnp.moveaxis(section, 0, dim))
        at += t[0].size
    return tuple(outs)


def sent_to_all(array, axis):
    peers = lax.axis_size(axis)
    return lax.all_to_all(
        jnp.broadcast_to(array[None], (peers, *array.shape)), axis, 0, 0, tiled=True
    )


def of_everyone(array, axis):
    everything = sent_to_all(array, axis)
    return jnp.sum(everything, axis=0)


def sent_together(arrays, axis, split_dim, concat_dim, along):
    columns = [a.reshape(*a.shape[:along], -1) for a in arrays]
    both = jnp.concatenate(columns, axis=along)
    result, at, outs = (
        lax.all_to_all(both, axis, split_axis=split_dim, concat_axis=concat_dim, tiled=True),
        0,
        [],
    )
    for a, column in zip(arrays, columns):
        section = result[..., at : at + column.shape[along]]
        outs.append(section.reshape(*section.shape[:along], *a.shape[along:]))
        at += column.shape[along]
    return tuple(outs)


def in_blocks(array, dim, peers):
    shape = array.shape
    parts = array.reshape(*shape[:dim], peers, shape[dim] // peers, *shape[dim + 1 :])
    return jnp.moveaxis(parts, dim, 0)


def sent_and_summed(array, axis, dim):
    peers = lax.axis_size(axis)
    parts = lax.all_to_all(in_blocks(array, dim, peers), axis, 0, 0, tiled=True)
    return jnp.sum(parts.astype(jnp.float32), axis=0)


def shards(
    teacher_in,
    teacher_attn,
    teacher_out_proj,
    teacher_gain,
    projection,
    student_in,
    student_attn,
    student_out_proj,
    student_gain,
    token_ids,
    row_order,
):
    student_count = lax.axis_size("student")
    teacher_count = lax.axis_size("teacher")
    row_count = teacher_in.shape[0]
    piece_rows = row_count // student_count
    student_index = lax.axis_index("student")
    attn_all = lax.all_gather(teacher_attn, "teacher", axis=1, tiled=True)
    out_full, proj_full = rows_first((teacher_out_proj, projection), "student", (0, 1))
    branch = jnp.dot(attn_all, out_full, preferred_element_type=jnp.float32)
    residual = teacher_in.astype(jnp.float32) + branch
    square_sum = of_everyone(jnp.sum(residual * residual, axis=1), "teacher")
    teacher_scale = lax.rsqrt(square_sum / DT + epsilon)
    hidden = (residual * teacher_scale[:, None] * teacher_gain.astype(jnp.float32)[None, :]).astype(
        jnp.bfloat16
    )
    proj_blocks = proj_full.reshape(
        proj_full.shape[0], teacher_count, proj_full.shape[1] // teacher_count
    )
    row_blocks = row_order.reshape(student_count, student_count, piece_rows)
    local_rows = (
        lax.dynamic_index_in_dim(row_blocks, student_index, 1, keepdims=False)
        - student_index * row_count
    )
    live_rows = jnp.where(token_ids != PAD_ID, 1.0, 0.0).astype(jnp.bfloat16)
    mask_send = jnp.take(live_rows, local_rows, axis=0)
    columns = proj_blocks
    summed = lax.psum_scatter(
        jnp.einsum("tf,fko->kto", hidden, columns, preferred_element_type=jnp.float32).astype(
            jnp.bfloat16
        ),
        "teacher",
        scatter_dimension=0,
        tiled=True,
    ).astype(jnp.float32)
    target_rows = summed[0].astype(jnp.bfloat16)
    moved, mask_got = sent_together(
        (jnp.take(target_rows, local_rows, axis=0), mask_send), "student", 0, 0, 2
    )
    target = moved.reshape(row_count, moved.shape[2])
    weight_mask = mask_got.reshape(row_count).astype(jnp.float32)
    attn_student = lax.all_gather(student_attn, "teacher", axis=1, tiled=True)
    columns = attn_student
    student_branch = jnp.dot(
        columns,
        lax.all_gather(student_out_proj, "student", axis=0, tiled=True),
        preferred_element_type=jnp.float32,
    )
    student_res = student_in.astype(jnp.float32) + student_branch
    student_square = of_everyone(jnp.sum(student_res * student_res, axis=1), "teacher")
    student_scale = lax.rsqrt(student_square / DS + epsilon)
    normed = student_res * student_scale[:, None]
    gain_values = student_gain.astype(jnp.float32)[None, :]
    distance = normed * gain_values - target.astype(jnp.float32)
    loss_weight = 1.0 / math.sqrt(row_count * student_count)
    grad_out = distance * (weight_mask * loss_weight)[:, None]
    gain_part = jnp.sum(grad_out * normed, axis=0)
    grad_norm = grad_out * gain_values
    inner_sum = of_everyone(jnp.sum(grad_norm * normed, axis=1), "teacher")
    grad_res = (student_scale[:, None] * (grad_norm - normed * (inner_sum / DS)[:, None])).astype(
        jnp.bfloat16
    )
    columns = attn_student
    grad_weight = sent_and_summed(
        lax.dot_general(
            columns, grad_res, (((0,), (0,)), ((), ())), preferred_element_type=jnp.float32
        ).astype(jnp.bfloat16),
        "student",
        0,
    )
    grad_gain = of_everyone(gain_part, "student")
    return (grad_weight, grad_gain)


def solution(mesh):
    placed = (
        P("student", "teacher"),
        P("student", "teacher"),
        P("student", "teacher"),
        P("teacher"),
        P("teacher", "student"),
        P("student", "teacher"),
        P("student", "teacher"),
        P("student", "teacher"),
        P("teacher"),
        P("student"),
        P(),
    )
    return jax.shard_map(
        shards,
        mesh=mesh,
        in_specs=placed,
        out_specs=(P("student", "teacher"), P("teacher")),
        check_vma=False,
    )
```

profile of v0, /device:TPU:1, one launch (start us, length us, event | category | flops | bytes accessed | tf_op | source)
XLA Modules:
  0.0 564.7 jit_solution(5684495137640013331)
XLA Ops:
  11.7 2.6 copy.62
  14.3 117.4 %all-gather.11.cloned.1.call-done = bf16[1024,4096]{1,0:T(8,128)(2,1)} async-done(((bf16[1024,512]{1,0:T(8,128)(2,1)}), bf16[1024,4096]{1,0:T(8,128)(2,1)}) %all-gather.11.cloned.1.call-update) | async-done | bytes 8388624 | tf_op jit(solution)/shard_map/all_gather | solution.py:84
  131.7 99.9 %all-gather.9.cloned.1.call-done = bf16[4096,2048]{0,1:T(8,128)(2,1)} async-done(((bf16[256,2048]{0,1:T(8,128)(2,1)}), bf16[4096,2048]{0,1:T(8,128)(2,1)}) %all-gather.9.cloned.1.call-update) | async-done | bytes 16777232 | tf_op jit(solution)/shard_map/all_gather | solution.py:19
  231.5 15.5 %multiply_reduce_fusion = (f32[1024]{0:T(1024)S(1)}, f32[1024,1024]{1,0:T(8,128)}) fusion(bf16[1024,1024]{0,1:T(8,128)(2,1)} %copy.62, bf16[1024,4096]{1,0:T(8,128)(2,1)} %all-gather.11.cloned.1.call-done, bf16[4096,2048]{0,1:T(8,128)(2,1)} %all-gather.9.cloned.1.call-done), kind=kOutput, calls=%fused_computation.9 | convolution fusion | flops 8594127872 | bytes 23072768 | tf_op jit(solution)/shard_map/dot_general | solution.py:86
  247.6 6.3 %all-to-all-start.1 = ((f32[8,1,1024]{2,1,0:T(1,128)}), f32[8,1,1024]{2,1,0:T(1,128)S(1)}, u32[]{:S(2)}, u32[]{:S(2)}) async-start(f32[8,1,1024]{2,1,0:T(1,128)} %broadcast_in_dim.34), calls=%async_computation.1 | async-start | bytes 65536 | tf_op jit(solution)/shard_map/all_to_all | solution.py:29
  254.1 7.8 %slice_bitcast_fusion = bf16[1024,4096]{1,0:T(8,128)(2,1)} fusion(bf16[4096,2048]{0,1:T(8,128)(2,1)} %all-gather.9.cloned.1.call-done), kind=kLoop, calls=%fused_computation.4 | loop fusion | bytes 16777216 | tf_op jit(solution)/shard_map/transpose | solution.py:22
  261.9 12.1 %copy.61 = bf16[1024,4096]{0,1:T(8,128)(2,1)} copy(bf16[1024,4096]{1,0:T(8,128)(2,1)} %slice_bitcast_fusion) | data formatting | bytes 16777216 | tf_op jit(solution)/shard_map/transpose | solution.py:22
  274.1 15.4 %convert_bitcast_fusion = bf16[8,1024,512]{1,2,0:T(8,128)(2,1)} fusion(bf16[1024,8,512]{0,2,1:T(8,128)(2,1)} %bitcast.38, f32[1024,1024]{1,0:T(8,128)} %get-tuple-element.11, bf16[1024,1024]{0,1:T(8,128)(2,1)S(1)} %copy-done.1, f32[1024]{0:T(1024)S(1)} %convert_element_type.58, f32[1024]{0:T(1024)S(1)} %add_rsqrt_fusion), kind=kOutput, calls=%fused_computation.5 | convolution fusion | flops 8599371776 | bytes 23076864 | tf_op jit(solution)/shard_map/tf,fko->kto/dot_general | solution.py:105
  290.6 6.8 %gather_fusion.1 = bf16[1024]{0:T(1024)(128)(2,1)S(1)} fusion(bf16[1024]{0:T(1024)(128)(2,1)S(1)} %select_convert_fusion, s32[1024]{0:T(1024)S(1)} %broadcast_clamp_fusion), kind=kCustom, calls=%fused_computation.1 | custom fusion | bytes 8192 | tf_op jit(solution)/shard_map/jit(_take)/gather | solution.py:102
  298.3 46.4 %all-gather.5.cloned.1.call-done = bf16[1024,2048]{1,0:T(8,128)(2,1)} async-done(((bf16[1024,256]{1,0:T(8,128)(2,1)}), bf16[1024,2048]{1,0:T(8,128)(2,1)}) %all-gather.5.cloned.1.call-update) | async-done | bytes 4194320 | tf_op jit(solution)/shard_map/all_gather | solution.py:118
  344.7 6.6 %multiply_reduce_fusion.3 = (f32[1024]{0:T(1024)S(1)}, f32[1024,512]{0,1:T(8,128)}) fusion(bf16[1024,2048]{1,0:T(8,128)(2,1)} %all-gather.5.cloned.1.call-done, bf16[2048,512]{1,0:T(8,128)(2,1)} %all-gather.7.cloned.1.call-done, bf16[1024,512]{0,1:T(8,128)(2,1)S(1)} %copy.58), kind=kOutput, calls=%fused_computation.19 | convolution fusion | flops 2149579776 | bytes 9441280 | tf_op jit(solution)/shard_map/dot_general | solution.py:120
  351.9 3.4 all-to-all-start
  355.3 107.1 %reduce-scatter.2.cloned.1.call-done = bf16[1,1024,512]{1,2,0:T(8,128)(2,1)} async-done(((bf16[8,1024,512]{1,2,0:T(8,128)(2,1)}), bf16[1,1024,512]{1,2,0:T(8,128)(2,1)}) %reduce-scatter.2.cloned.1.call-update) | async-done | bytes 1048592 | tf_op jit(solution)/shard_map/reduce_scatter | solution.py:104
  463.9 4.0 gather_fusion
  469.3 5.8 %all-to-all-start.2 = ((bf16[16,64,513]{2,1,0:T(8,128)(2,1)}), bf16[16,64,513]{2,1,0:T(8,128)(2,1)S(1)}, u32[]{:S(2)}, u32[]{:S(2)}) async-start(bf16[16,64,513]{2,1,0:T(8,128)(2,1)} %pad_maximum_fusion), calls=%async_computation.3 | async-start | bytes 2621440 | tf_op jit(solution)/shard_map/all_to_all | solution.py:43
  475.1 18.5 %all-to-all-done.2 = bf16[16,64,513]{2,1,0:T(8,128)(2,1)S(1)} async-done(((bf16[16,64,513]{2,1,0:T(8,128)(2,1)}), bf16[16,64,513]{2,1,0:T(8,128)(2,1)S(1)}, u32[]{:S(2)}, u32[]{:S(2)}) %all-to-all-start.2) | async-done | bytes 1050656 | tf_op jit(solution)/shard_map/all_to_all | solution.py:43
  495.4 1.9 copy.67
  497.6 2.4 multiply_reduce_fusion.1
  500.0 10.2 %all_to_all.34 = f32[8,1,1024]{2,1,0:T(1,128)S(1)} all-to-all(f32[8,1,1024]{2,1,0:T(1,128)S(1)} %broadcast_in_dim.62), channel_id=1, replica_groups=mesh['teacher'=8,'student'=16] {'teacher'}, dimensions={0} | all-to-all | bytes 65536 | tf_op jit(solution)/shard_map/all_to_all | solution.py:29
  510.8 5.5 all-to-all-start.5
  516.4 5.4 fusion.6
  521.8 1.9 copy.82
  523.6 5.8 %all-to-all-start.4 = ((bf16[16,128,512]{1,2,0:T(8,128)(2,1)}), bf16[16,128,512]{1,2,0:T(8,128)(2,1)S(1)}, u32[]{:S(2)}, u32[]{:S(2)}) async-start(bf16[16,128,512]{1,2,0:T(8,128)(2,1)} %bitcast.37), calls=%async_computation.5 | async-start | bytes 4194304 | tf_op jit(solution)/shard_map/all_to_all | solution.py:62
  530.0 27.0 %all-to-all-done.4 = bf16[16,128,512]{1,2,0:T(8,128)(2,1)S(1)} async-done(((bf16[16,128,512]{1,2,0:T(8,128)(2,1)}), bf16[16,128,512]{1,2,0:T(8,128)(2,1)S(1)}, u32[]{:S(2)}, u32[]{:S(2)}) %all-to-all-start.4) | async-done | bytes 2097184 | tf_op jit(solution)/shard_map/all_to_all | solution.py:62
  (65 shorter events, 15.3 us)
Async XLA Ops:
  7.2 2.1 copy-start.3
  7.2 124.5 %all-gather.11.cloned.1.call-start = ((), (), s32[]{:S(2)}) async-start(), calls=%async_computation.10 | async-start | bytes 9437184 | tf_op jit(solution)/shard_map/all_gather | solution.py:84
  7.9 223.6 %all-gather.9.cloned.1.call-start = ((), (), s32[]{:S(2)}) async-start(), calls=%async_computation.9 | async-start | bytes 17825792 | tf_op jit(solution)/shard_map/all_gather | solution.py:19
  9.2 2.5 copy-start
  10.4 288.0 %all-gather.7.cloned.1.call-start = ((), (), s32[]{:S(2)}) async-start(), calls=%async_computation.8 | async-start | bytes 2228224 | tf_op jit(solution)/shard_map/all_gather | solution.py:122
  11.1 333.6 %all-gather.5.cloned.1.call-start = ((), (), s32[]{:S(2)}) async-start(), calls=%async_computation.7 | async-start | bytes 4718592 | tf_op jit(solution)/shard_map/all_gather | solution.py:118
  11.7 2.6 copy-start.6
  247.6 26.5 %all-to-all-start.1 = ((f32[8,1,1024]{2,1,0:T(1,128)}), f32[8,1,1024]{2,1,0:T(1,128)S(1)}, u32[]{:S(2)}, u32[]{:S(2)}) async-start(f32[8,1,1024]{2,1,0:T(1,128)} %broadcast_in_dim.34), calls=%async_computation.1 | async-start | bytes 65536 | tf_op jit(solution)/shard_map/all_to_all | solution.py:29
  253.9 208.5 %reduce-scatter.2.cloned.1.call-start = ((), (), s32[]{:S(2)}) async-start(), calls=%async_computation.11 | async-start | bytes 9437184 | tf_op jit(solution)/shard_map/reduce_scatter | solution.py:104
  261.9 12.2 %copy-start.1 = (bf16[1024,1024]{0,1:T(8,128)(2,1)S(1)}, bf16[1024,1024]{0,1:T(8,128)(2,1)}, u32[]{:S(2)}) copy-start(bf16[1024,1024]{0,1:T(8,128)(2,1)} %copy.62) | copy-start | bytes 6291460
  289.5 0.8 copy-start.4
  289.5 1.0 copy-start.5
  290.6 7.1 %copy-start.2 = (bf16[1024,512]{1,0:T(8,128)(2,1)S(1)}, bf16[1024,512]{1,0:T(8,128)(2,1)}, u32[]{:S(2)}) copy-start(bf16[1024,512]{1,0:T(8,128)(2,1)} %param.16) | copy-start | bytes 3145732
  351.9 117.4 %all-to-all-start = ((f32[8,1,1024]{2,1,0:T(1,128)}), f32[8,1,1024]{2,1,0:T(1,128)S(1)}, u32[]{:S(2)}, u32[]{:S(2)}) async-start(f32[8,1,1024]{2,1,0:T(1,128)} %broadcast_in_dim.32), calls=%async_computation | async-start | bytes 65536 | tf_op jit(solution)/shard_map/all_to_all | solution.py:29
  468.1 7.0 %copy-start.7 = (bf16[512]{0:T(512)(128)(2,1)S(1)}, bf16[512]{0:T(512)(128)(2,1)}, u32[]{:S(2)}) copy-start(bf16[512]{0:T(512)(128)(2,1)} %param.19) | copy-start | bytes 3076
  469.3 24.3 %all-to-all-start.2 = ((bf16[16,64,513]{2,1,0:T(8,128)(2,1)}), bf16[16,64,513]{2,1,0:T(8,128)(2,1)S(1)}, u32[]{:S(2)}, u32[]{:S(2)}) async-start(bf16[16,64,513]{2,1,0:T(8,128)(2,1)} %pad_maximum_fusion), calls=%async_computation.3 | async-start | bytes 2621440 | tf_op jit(solution)/shard_map/all_to_all | solution.py:43
  510.8 12.8 %all-to-all-start.5 = ((f32[16,1,512]{2,1,0:T(1,128)}), f32[16,1,512]{2,1,0:T(1,128)S(1)}, u32[]{:S(2)}, u32[]{:S(2)}) async-start(f32[16,1,512]{2,1,0:T(1,128)} %broadcast_in_dim.63), calls=%async_computation.6 | async-start | bytes 65536 | tf_op jit(solution)/shard_map/all_to_all | solution.py:29
  523.6 33.4 %all-to-all-start.4 = ((bf16[16,128,512]{1,2,0:T(8,128)(2,1)}), bf16[16,128,512]{1,2,0:T(8,128)(2,1)S(1)}, u32[]{:S(2)}, u32[]{:S(2)}) async-start(bf16[16,128,512]{1,2,0:T(8,128)(2,1)} %bitcast.37), calls=%async_computation.5 | async-start | bytes 4194304 | tf_op jit(solution)/shard_map/all_to_all | solution.py:62
Sparse Core Ops, SparseCore 0:
  10.2 121.4 all-gather.10
  133.3 98.2 all-gather.8
  233.2 33.8 all-gather.6
  269.2 75.5 all-gather.4
  348.4 113.9 reduce-scatter.1
where the time goes:
time: 566 us; the launch traced here: 565 us
  waiting for transfers between devices  418 us (74%)
  local copies, waits for them, and re-layouts  44.6 us (8%)
  matrix products  42.8 us (8%)
  starting transfers between devices  27.1 us (5%)
  between operations  14 us (2%)
  blocking collectives  10.2 us (2%)
  other arithmetic  7.84 us (1%)
    all_gather x1, waiting for transfers between devices, shards(): attn_all = lax.all_gather(teacher_attn, 'teacher', axis=1, tiled=True)  117 us
    reduce_scatter x1, waiting for transfers between devices, shards(): lax.psum_scatter(jnp.einsum('tf,fko->kto', hidden, columns, preferred_ele...  107 us
    all_gather x1, waiting for transfers between devices, rows_first(): result, at, outs = (lax.all_gather(both, axis, axis=0, tiled=True), 0, [])  99.9 us
    all_gather x1, waiting for transfers between devices, shards(): attn_student = lax.all_gather(student_attn, 'teacher', axis=1, tiled=True)  46.4 us
    all_to_all x1, waiting for transfers between devices, sent_and_summed(): parts = lax.all_to_all(in_blocks(array, dim, peers), axis, 0, 0, tiled=True)  27 us
    transpose x2, local copies, waits for them, and re-layouts, rows_first(): outs.append(jnp.moveaxis(section, 0, dim))  19.9 us
    all_to_all x1, waiting for transfers between devices, sent_together(): lax.all_to_all(both, axis, split_axis=split_dim, concat_axis=concat_dim,...  18.5 us
    dot_general x1, matrix products, shards(): branch = jnp.dot(attn_all, out_full, preferred_element_type=jnp.float32)  15.5 us
  transfers between devices with their start and end apart: 10, of which 6 were waited for; matrix products, arithmetic and copies ran while one was open for 15% of the time, Pallas kernels for 0%

commit v1 on v0

v1 whole, which is shorter than its diff:
```python
import math

import jax
import jax.numpy as jnp
from jax import lax
from jax.experimental import pallas as pl
from jax.experimental.pallas import tpu as pltpu
from jax.sharding import PartitionSpec as P

DT = 8192
DS = 4096
PAD_ID = 128004
epsilon = 1e-05

BF = jnp.bfloat16
F32 = jnp.float32
SLOTS = 160


def div(a, b):
    return lax.div(a, jnp.int32(b))


def rem(a, b):
    return lax.rem(a, jnp.int32(b))


class Place:
    def __init__(self):
        t = lax.axis_index("teacher")
        s = lax.axis_index("student")
        self.t, self.s = t, s
        self.zh, self.y = div(t, 4), rem(t, 4)
        self.zl, self.x, self.core = div(s, 8), rem(div(s, 2), 4), rem(s, 2)
        self.z = self.zh * 2 + self.zl

    def dev(self, dz=0, dy=0, dx=0, dc=0):
        t, s = self.index(dz, dy, dx, dc)
        return {"teacher": t, "student": s}

    def index(self, dz=0, dy=0, dx=0, dc=0):
        z, y, x, c = self.z, self.y, self.x, self.core
        if dz:
            z = rem(z + (dz % 4), 4)
        if dy:
            y = rem(y + (dy % 4), 4)
        if dx:
            x = rem(x + (dx % 4), 4)
        if dc:
            c = 1 - c
        return div(z, 2) * 4 + y, rem(z, 2) * 8 + x * 2 + c


class Net:
    def __init__(self, send, recv):
        self.send, self.recv, self.n, self.open = send, recv, 0, []

    def copy(self, src, dst, device):
        c = pltpu.make_async_remote_copy(
            src_ref=src,
            dst_ref=dst,
            send_sem=self.send.at[self.n],
            recv_sem=self.recv.at[self.n],
            device_id=device,
            device_id_type=pl.DeviceIdType.MESH,
        )
        self.n += 1
        c.start()
        self.open.append(c)
        return c

    def sent(self, copies):
        for c in copies:
            c.wait_send()
        gone = {id(c) for c in copies}
        self.open = [c for c in self.open if id(c) not in gone]

    def finish(self):
        for c in self.open:
            c.wait_send()
        self.open = []


def got(*copies):
    for c in copies:
        c.wait_recv()


def gather_kernel(
    tin, tattn, tw, tgain, proj, sin, sattn, su,
    target_out, sq_out, sres_out, attn_out, ssq_out,
    bufA, bufC, bufW, bufP, bufU, tinv, sinv, hid,
    tmpA, tmpC, tmpE, r1, r2, r3, zs,
    send, recv, local,
):
    p = Place()
    up, down = {"dy": 1}, {"dy": -1}
    barrier = pltpu.get_barrier_semaphore()
    near = [dict(dy=1), dict(dy=-1), dict(dz=1), dict(dz=-1), dict(dx=1), dict(dx=-1), dict(dc=1)]
    for n in near:
        pl.semaphore_signal(barrier, inc=1, device_id=p.dev(**n), device_id_type=pl.DeviceIdType.MESH)
    pl.semaphore_wait(barrier, len(near))
    net = Net(send, recv)

    A = (tattn, bufA, tmpA, 512)
    C = (sattn, bufC, tmpC, 512)
    W = (tw, bufW, 128)
    Q = (proj, bufP, 512)
    U = (su, bufU, 64)

    def own(arr, h):
        half = arr[-1]
        return arr[0].at[pl.ds(h * half, half), :]

    def slot(arr, i, h):
        half = arr[-1]
        return arr[1].at[i, pl.ds(h * half, half), :]

    tp = p.index(dz=2)[0]
    zpart = {"teacher": p.t, "student": rem(p.s + 8, 16)}
    sp = rem(p.s + 8, 16)
    sib = p.dev(dc=1)
    sib_index = p.index(dc=1)[1]
    locals_ = []

    def bring(src, dst):
        c = pltpu.make_async_copy(src, dst, local.at[len(locals_)])
        c.start()
        locals_.append(c)
        return c

    def t_own(arr):
        ups = [net.copy(own(arr, h), slot(arr, p.t, h), p.dev(dy=1)) for h in (0, 1)]
        downs = [net.copy(own(arr, h), slot(arr, p.t, h), p.dev(dy=-1)) for h in (1, 0)][::-1]
        return ups, downs

    def t_hop1(arr):
        return [
            net.copy(own(arr, 0), arr[2].at[0], p.dev(dz=1)),
            net.copy(own(arr, 1), arr[2].at[1], p.dev(dz=-1)),
        ]

    def t_hop2(arr, hop1):
        got(hop1[0])
        a = net.copy(arr[2].at[0], slot(arr, p.index(dz=-1)[0], 0), p.dev(dz=1))
        got(hop1[1])
        b = net.copy(arr[2].at[1], slot(arr, p.index(dz=1)[0], 1), p.dev(dz=-1))
        return [a, b]

    def t_forward(arr, ups, downs, dz):
        got(ups[0])
        a = net.copy(slot(arr, p.index(dz=dz, dy=-1)[0], 0), slot(arr, p.index(dz=dz, dy=-1)[0], 0), p.dev(dy=1))
        got(downs[1])
        b = net.copy(slot(arr, p.index(dz=dz, dy=1)[0], 1), slot(arr, p.index(dz=dz, dy=1)[0], 1), p.dev(dy=-1))
        return [a, b]

    def t_partner(arr, hop2):
        got(*hop2)
        ups = [net.copy(slot(arr, tp, h), slot(arr, tp, h), p.dev(dy=1)) for h in (0, 1)]
        downs = [net.copy(slot(arr, tp, h), slot(arr, tp, h), p.dev(dy=-1)) for h in (1, 0)][::-1]
        return ups, downs

    def s_own(arr):
        ups = [net.copy(own(arr, h), slot(arr, p.s, h), p.dev(dx=1)) for h in (0, 1)]
        downs = [net.copy(own(arr, h), slot(arr, p.s, h), p.dev(dx=-1)) for h in (1, 0)][::-1]
        return ups, downs

    def s_side(arr):
        return net.copy(arr[0], arr[1].at[p.s], zpart)

    def s_partner(arr, side):
        got(side)
        ups = [net.copy(slot(arr, sp, h), slot(arr, sp, h), p.dev(dx=1)) for h in (0, 1)]
        downs = [net.copy(slot(arr, sp, h), slot(arr, sp, h), p.dev(dx=-1)) for h in (1, 0)][::-1]
        return ups, downs

    def s_index(dx, other):
        i = p.index(dx=dx)[1]
        return rem(i + 8, 16) if other else i

    def s_forward(arr, ups, downs, other):
        got(ups[0])
        i = s_index(-1, other)
        a = net.copy(slot(arr, i, 0), slot(arr, i, 0), p.dev(dx=1))
        got(downs[1])
        j = s_index(1, other)
        b = net.copy(slot(arr, j, 1), slot(arr, j, 1), p.dev(dx=-1))
        return [a, b]

    def share(arr, i):
        return net.copy(arr[1].at[i], arr[1].at[i], sib)

    ssides, sowns, shared = {}, {}, []
    aown = t_own(A)
    ahop1 = t_hop1(A)
    for n, arr in (("W", W), ("Q", Q)):
        sowns[n] = s_own(arr)
        ssides[n] = s_side(arr)
        shared.append(net.copy(arr[0], arr[1].at[p.s], sib))
    bring(tattn, bufA.at[p.t])
    bring(tw, bufW.at[p.s])
    bring(proj, bufP.at[p.s])
    bring(tin, tinv)
    bring(sattn, bufC.at[p.t])
    bring(su, bufU.at[p.s])
    bring(sin, sinv)
    cown = t_own(C)

    ahop2 = t_hop2(A, ahop1)
    chop1 = t_hop1(C)
    sowns["U"] = s_own(U)
    ssides["U"] = s_side(U)
    shared.append(net.copy(U[0], U[1].at[p.s], sib))
    S = (("W", W), ("Q", Q), ("U", U))
    sfwd, sfwd2, sparts = {}, {}, {}
    for n, arr in S[:2]:
        sfwd[n] = s_forward(arr, *sowns[n], False)
    afwd = t_forward(A, *aown, 0)
    for n, arr in S[:2]:
        sparts[n] = s_partner(arr, ssides[n])
    apart = t_partner(A, ahop2)
    chop2 = t_hop2(C, chop1)
    for n, arr in S[:2]:
        got(sowns[n][0][1], sowns[n][1][0])
        shared.append(share(arr, sp))
        shared.append(share(arr, s_index(-1, False)))
        shared.append(share(arr, s_index(1, False)))
    sfwd["U"] = s_forward(U, *sowns["U"], False)
    sparts["U"] = s_partner(U, ssides["U"])
    for n, arr in S[:2]:
        sfwd2[n] = s_forward(arr, *sparts[n], True)
    afwd2 = t_forward(A, *apart, 2)
    cfwd = t_forward(C, *cown, 0)
    cpart = t_partner(C, chop2)
    for n, arr in S[:2]:
        got(*sfwd[n], sparts[n][0][1], sparts[n][1][0])
        shared.append(share(arr, s_index(2, False)))
        shared.append(share(arr, s_index(-1, True)))
        shared.append(share(arr, s_index(1, True)))
    sfwd2["U"] = s_forward(U, *sparts["U"], True)
    for n, arr in S[:2]:
        got(*sfwd2[n])
        shared.append(share(arr, s_index(2, True)))
    got(sowns["U"][0][1], sowns["U"][1][0], sparts["U"][0][1], sparts["U"][1][0], *sfwd["U"])
    ushared = [
        share(U, sp),
        share(U, s_index(-1, False)),
        share(U, s_index(1, False)),
        share(U, s_index(2, False)),
        share(U, s_index(-1, True)),
        share(U, s_index(1, True)),
    ]
    got(aown[0][1], aown[1][0], *afwd, apart[0][1], apart[1][0], *afwd2)
    got(*shared)
    for c in locals_:
        c.wait()

    sq_out[...] = jnp.zeros_like(sq_out)

    def first(i, carry):
        rows = pl.ds(pl.multiple_of(div(i, 2) * 512, 512), 512)
        cols = pl.ds(pl.multiple_of(rem(i, 2) * 512, 512), 512)
        acc = tinv[rows, cols].astype(F32)
        for t in range(8):
            w = bufW[2 * t : 2 * t + 2, :, cols].reshape(512, 512)
            acc = acc + jnp.dot(bufA[t, rows, :], w, preferred_element_type=F32)
        square = acc * acc
        sq_out[rows, :] += square[:, 0:128] + square[:, 128:256] + square[:, 256:384] + square[:, 384:512]
        hid[rows, cols] = (acc * tgain[:, cols].astype(F32)).astype(BF)
        return carry

    lax.fori_loop(0, 2, first, 0)
    cfwd2 = t_forward(C, *cpart, 2)
    lax.fori_loop(2, 4, first, 0)
    net.sent([*aown[0], *aown[1], *ahop1, *ahop2, *afwd, *apart[0], *apart[1], *afwd2])

    def project(k):
        def step(i, carry):
            rows = pl.ds(pl.multiple_of(i * 512, 512), 512)
            h = hid[rows, :]
            bufA[k, rows, 0:256] = jnp.dot(h, bufP[2 * k], preferred_element_type=F32).astype(BF)
            bufA[k, rows, 256:512] = jnp.dot(h, bufP[2 * k + 1], preferred_element_type=F32).astype(BF)
            return carry

        lax.fori_loop(0, 2, step, 0)

    def block(far, dy):
        zh = 1 - p.zh if far else p.zh
        y = rem(p.y + (dy % 4), 4)
        return zh * 4 + y

    lo, hi = pl.ds(0, 512), pl.ds(512, 512)

    def opening(n, far):
        k = block(far, 2)
        project(k)
        return (
            net.copy(bufA.at[k, lo, :], r1.at[n, 0], p.dev(dy=1)),
            net.copy(bufA.at[k, hi, :], r1.at[n, 1], p.dev(dy=-1)),
        )

    def plain(n, far):
        ku, kd = block(far, 1), block(far, -1)
        project(ku)
        u = net.copy(bufA.at[ku, hi, :], r2.at[n, 0, hi, :], p.dev(dy=1))
        project(kd)
        d = net.copy(bufA.at[kd, lo, :], r2.at[n, 1, lo, :], p.dev(dy=-1))
        return u, d

    def added(n, far, opened):
        ku, kd = block(far, 1), block(far, -1)

        def add(k, base, j):
            def step(i, carry):
                at = pl.ds(pl.multiple_of(i * 128, 128), 128)
                rows = pl.ds(pl.multiple_of(base + i * 128, 128), 128)
                bufA[k, rows, :] = (bufA[k, rows, :].astype(F32) + r1[n, j, at, :].astype(F32)).astype(BF)
                return carry

            lax.fori_loop(0, 4, step, 0)

        got(opened[0])
        add(ku, 0, 0)
        u = net.copy(bufA.at[ku, lo, :], r2.at[n, 0, lo, :], p.dev(dy=1))
        got(opened[1])
        add(kd, 512, 1)
        d = net.copy(bufA.at[kd, hi, :], r2.at[n, 1, hi, :], p.dev(dy=-1))
        return u, d

    open_far = opening(0, True)
    plain_far = plain(0, True)
    open_near = opening(1, False)
    added_far = added(0, True, open_far)
    plain_near = plain(1, False)
    added_near = added(1, False, open_near)
    k_far, k_near = block(True, 0), block(False, 0)
    project(k_far)
    project(k_near)

    got(cown[0][1], cown[1][0], *cfwd, cpart[0][1], cpart[1][0], *cfwd2)
    got(*sfwd2["U"])
    ushared.append(share(U, s_index(2, True)))
    got(*ushared)
    outs = []
    for t in range(8):
        c = pltpu.make_async_copy(
            bufC.at[t], attn_out.at[:, pl.ds(t * 256, 256)], local.at[len(locals_) + t]
        )
        c.start()
        outs.append(c)

    def student(i, carry):
        rows = pl.ds(pl.multiple_of(i * 512, 512), 512)
        acc = sinv[rows, :].astype(F32)
        for t in range(8):
            w = bufU[2 * t : 2 * t + 2].reshape(256, 512)
            acc = acc + jnp.dot(bufC[t, rows, :], w, preferred_element_type=F32)
        square = acc * acc
        ssq_out[rows, :] = square[:, 0:128] + square[:, 128:256] + square[:, 256:384] + square[:, 384:512]
        sres_out[rows, :] = acc
        return carry

    lax.fori_loop(0, 2, student, 0)

    def three(n, k, base, i):
        at = pl.ds(pl.multiple_of(base + i * 128, 128), 128)
        return at, (
            bufA[k, at, :].astype(F32) + r2[n, 0, at, :].astype(F32) + r2[n, 1, at, :].astype(F32)
        )

    got(*plain_far, *added_far)

    def far_sum(i, carry):
        at, total = three(0, k_far, 0, i)
        zs[at, :] = total.astype(BF)
        return carry

    lax.fori_loop(0, 8, far_sum, 0)
    hop1 = (
        net.copy(zs.at[lo, :], tmpE.at[0], p.dev(dz=1)),
        net.copy(zs.at[hi, :], tmpE.at[1], p.dev(dz=-1)),
    )
    got(hop1[0])
    h2a = net.copy(tmpE.at[0], r3.at[lo, :], p.dev(dz=1))
    got(hop1[1])
    h2b = net.copy(tmpE.at[1], r3.at[hi, :], p.dev(dz=-1))
    got(*plain_near, *added_near)
    got(h2a, h2b)

    def near_sum(i, carry):
        at, total = three(1, k_near, 0, i)
        target_out[at, :] = (total + r3[at, :].astype(F32)).astype(BF)
        return carry

    lax.fori_loop(0, 8, near_sum, 0)
    for c in outs:
        c.wait()
    net.finish()


def gathered(tin, tattn, tw, tgain, proj, sin, sattn, su):
    anywhere = pl.BlockSpec(memory_space=pl.ANY)
    vmem = pl.BlockSpec(memory_space=pltpu.VMEM)
    V = pltpu.VMEM
    return pl.pallas_call(
        gather_kernel,
        out_shape=(
            jax.ShapeDtypeStruct((1024, 512), BF),
            jax.ShapeDtypeStruct((1024, 128), F32),
            jax.ShapeDtypeStruct((1024, 512), F32),
            jax.ShapeDtypeStruct((1024, 2048), BF),
            jax.ShapeDtypeStruct((1024, 128), F32),
        ),
        in_specs=[anywhere, anywhere, anywhere, vmem, anywhere, anywhere, anywhere, anywhere],
        out_specs=(vmem, vmem, vmem, anywhere, vmem),
        scratch_shapes=[
            V((8, 1024, 512), BF),
            V((8, 1024, 256), BF),
            V((16, 256, 1024), BF),
            V((16, 1024, 256), BF),
            V((16, 128, 512), BF),
            V((1024, 1024), BF),
            V((1024, 512), BF),
            V((1024, 1024), BF),
            V((2, 512, 512), BF),
            V((2, 512, 256), BF),
            V((2, 512, 512), BF),
            V((2, 2, 512, 512), BF),
            V((2, 2, 1024, 512), BF),
            V((1024, 512), BF),
            V((1024, 512), BF),
            pltpu.SemaphoreType.DMA((SLOTS,)),
            pltpu.SemaphoreType.DMA((SLOTS,)),
            pltpu.SemaphoreType.DMA((16,)),
        ],
        compiler_params=pltpu.CompilerParams(
            collective_id=0, has_side_effects=True, vmem_limit_bytes=67043328
        ),
        name="gathered",
    )(tin, tattn, tw, tgain.reshape(1, -1), proj, sin, sattn, su)


def sent_to_all(array, axis):
    peers = lax.axis_size(axis)
    return lax.all_to_all(
        jnp.broadcast_to(array[None], (peers, *array.shape)), axis, 0, 0, tiled=True
    )


def of_everyone(array, axis):
    return jnp.sum(sent_to_all(array, axis), axis=0)


def shards(tin, tattn, tw, tgain, proj, sin, sattn, su, sgain, token_ids, row_order):
    s = lax.axis_index("student")
    row_count = 1024
    target_raw, sq, student_res, attn_student, ssq = gathered(
        tin, tattn, tw, tgain, proj, sin, sattn, su
    )
    sums = of_everyone(jnp.stack([jnp.sum(sq, axis=1), jnp.sum(ssq, axis=1)]), "teacher")
    teacher_scale = lax.rsqrt(sums[0] / DT + epsilon)
    student_scale = lax.rsqrt(sums[1] / DS + epsilon)
    target_rows = (target_raw.astype(F32) * teacher_scale[:, None]).astype(BF)
    local_rows = lax.dynamic_index_in_dim(
        row_order.reshape(16, 16, 64), s, 1, keepdims=False
    ).reshape(1024) - s * row_count
    pick = (local_rows[:, None] == jnp.arange(1024)[None, :]).astype(BF)
    live_rows = jnp.where(token_ids != PAD_ID, 1.0, 0.0).astype(BF)
    both = jnp.concatenate([target_rows, jnp.broadcast_to(live_rows[:, None], (1024, 128))], axis=1)
    moved = lax.all_to_all(
        jnp.dot(pick, both, preferred_element_type=F32).astype(BF).reshape(16, 64, 640),
        "student", 0, 0, tiled=True,
    ).reshape(1024, 640)
    target = moved[:, :512].astype(F32)
    weight_mask = moved[:, 512].astype(F32)
    normed = student_res * student_scale[:, None]
    gain_values = sgain.astype(F32)[None, :]
    distance = normed * gain_values - target
    loss_weight = 1.0 / math.sqrt(16384)
    grad_out = distance * (weight_mask * loss_weight)[:, None]
    gain_part = jnp.sum(grad_out * normed, axis=0)
    grad_norm = grad_out * gain_values
    inner_sum = of_everyone(jnp.sum(grad_norm * normed, axis=1), "teacher")
    grad_res = (student_scale[:, None] * (grad_norm - normed * (inner_sum / DS)[:, None])).astype(BF)
    parts = lax.dot_general(
        attn_student, grad_res, (((0,), (0,)), ((), ())), preferred_element_type=F32
    ).astype(BF)
    grad_weight = jnp.sum(
        lax.all_to_all(parts.reshape(16, 128, 512), "student", 0, 0, tiled=True).astype(F32), axis=0
    )
    grad_gain = of_everyone(gain_part, "student")
    return (grad_weight, grad_gain)


def solution(mesh):
    placed = (
        P("student", "teacher"),
        P("student", "teacher"),
        P("student", "teacher"),
        P("teacher"),
        P("teacher", "student"),
        P("student", "teacher"),
        P("student", "teacher"),
        P("student", "teacher"),
        P("teacher"),
        P("student"),
        P(),
    )
    return jax.shard_map(
        shards,
        mesh=mesh,
        in_specs=placed,
        out_specs=(P("student", "teacher"), P("teacher")),
        check_vma=False,
    )
```

time: 566 us -> 289 us (0.51)
  waiting for transfers between devices: 418 us -> 50.6 us
  Pallas kernels: 0 us -> 181 us
  local copies, waits for them, and re-layouts: 44.6 us -> 3.77 us
  matrix products: 42.8 us -> 9.23 us
  between operations: 14 us -> 0.77 us
    all_gather x4 -> x0, waiting for transfers between devices: 264 us -> none  [the longest x1 117 us: shards(): attn_all = lax.all_gather(teacher_attn, 'teacher', axis=1, tiled=True)]
    pallas_call x0 -> x1, Pallas kernels: none -> 181 us  [gathered(): pl.pallas_call(gather_kernel, out_shape=(jax.ShapeDtypeStruct((1024, 512)...]
    reduce_scatter x1 -> x0, waiting for transfers between devices: 107 us -> none  [shards(): lax.psum_scatter(jnp.einsum('tf,fko->kto', hidden, columns, preferred_ele...]
    dot_general x4 -> x2, matrix products: 42.8 us -> 9.23 us  [the longest x1 6.17 us: shards(): lax.dot_general(attn_student, grad_res, (((0,), (0,)), ((), ())), preferr...]
    transpose x2 -> x0, local copies, waits for them, and re-layouts: 19.9 us -> none  [rows_first(): outs.append(jnp.moveaxis(section, 0, dim))]
    gather x3 -> x0, local copies, waits for them, and re-layouts: 10.8 us -> none  [the longest x2 6.88 us: shards(): mask_send = jnp.take(live_rows, local_rows, axis=0)]
    unnamed x20 -> x6, local copies, waits for them, and re-layouts: 6.04 us -> 0.01 us
    all_to_all x3 -> x2, starting transfers between devices: 15.2 us -> 10.8 us  [sent_to_all(): lax.all_to_all(jnp.broadcast_to(array[None], (peers, *array.shape)), axis...]
  transfers between devices with their start and end apart: 10 -> 4, of which waited for: 6 -> 3; matrix products, arithmetic and copies ran while one was open for 15% -> 3% of each run, Pallas kernels for 0% -> 0%
where the time goes in v1:
time: 289 us; the launch traced here: 288 us
  Pallas kernels  181 us (63%)
  waiting for transfers between devices  50.6 us (18%)
  starting transfers between devices  26.8 us (9%)
  matrix products  9.23 us (3%)
  blocking collectives  8.99 us (3%)
  other arithmetic  6.43 us (2%)
  local copies, waits for them, and re-layouts  3.77 us (1%)
    pallas_call x1, Pallas kernels, gathered(): pl.pallas_call(gather_kernel, out_shape=(jax.ShapeDtypeStruct((1024, 512)...  181 us
    all_to_all x1, waiting for transfers between devices, shards(): lax.all_to_all(parts.reshape(16, 128, 512), 'student', 0, 0, tiled=True)  27 us
    all_to_all x1, waiting for transfers between devices, shards(): lax.all_to_all(jnp.dot(pick, both, preferred_element_type=F32).astype(BF)...  18.7 us
    all_to_all x2, starting transfers between devices, sent_to_all(): lax.all_to_all(jnp.broadcast_to(array[None], (peers, *array.shape)), axis...  10.8 us
    all_to_all x1, starting transfers between devices, shards(): lax.all_to_all(jnp.dot(pick, both, preferred_element_type=F32).astype(BF)...  10.2 us
    all_to_all x1, blocking collectives, sent_to_all(): lax.all_to_all(jnp.broadcast_to(array[None], (peers, *array.shape)), axis...  8.99 us
    dot_general x1, matrix products, shards(): lax.dot_general(attn_student, grad_res, (((0,), (0,)), ((), ())), preferr...  6.17 us
    all_to_all x1, starting transfers between devices, shards(): lax.all_to_all(parts.reshape(16, 128, 512), 'student', 0, 0, tiled=True)  5.79 us
  transfers between devices with their start and end apart: 4, of which 3 were waited for; matrix products, arithmetic and copies ran while one was open for 3% of the time, Pallas kernels for 0%

profile of v1, /device:TPU:1, one launch (start us, length us, event | category | flops | bytes accessed | tf_op | source)
XLA Modules:
  0.0 288.0 jit_solution(16515863039599150301)
XLA Ops:
  0.6 1.3 reshape.70.tgain
  1.9 181.4 %gathered.1 = (bf16[1024,512]{1,0:T(8,128)(2,1)}, f32[1024,128]{1,0:T(8,128)}, f32[1024,512]{1,0:T(8,128)}, bf16[1024,2048]{1,0:T(8,128)(2,1)}, f32[1024,128]{1,0:T(8,128)}) custom-call(bf16[1024,1024]{1,0:T(8,128)(2,1)} %tin.1, bf16[1024,512]{1,0:T(8,128)(2,1)} %tattn.1, bf16[256,1024]{1,0:T(8,128)(2,1)} %tw.1, bf16[1,1024]{1,0:T(2,128)(2,1)} %reshape.70.tgain, ...), custom_call_target="tpu_custom_call" | custom-call | tf_op jit(solution)/shard_map/gathered/pallas_call | solution.py:405
  183.3 1.3 reduce_sum.72
  184.7 1.2 reduce_sum.73
  185.9 0.6 broadcast_in_dim.16
  186.6 5.5 %all-to-all-start = ((f32[8,2,1024]{2,1,0:T(2,128)}), f32[8,2,1024]{2,1,0:T(2,128)S(1)}, u32[]{:S(2)}, u32[]{:S(2)}) async-start(f32[8,2,1024]{2,1,0:T(2,128)} %broadcast_in_dim.16), calls=%async_computation | async-start | bytes 131072 | tf_op jit(solution)/shard_map/all_to_all | solution.py:445
  192.1 0.7 select_convert_fusion
  192.7 0.9 reshape.71
  193.8 5.0 %all-to-all-done = f32[8,2,1024]{2,1,0:T(2,128)S(1)} async-done(((f32[8,2,1024]{2,1,0:T(2,128)}), f32[8,2,1024]{2,1,0:T(2,128)S(1)}, u32[]{:S(2)}, u32[]{:S(2)}) %all-to-all-start) | async-done | bytes 65568 | tf_op jit(solution)/shard_map/all_to_all | solution.py:445
  198.8 0.3 multiply_convert_fusion.1
  199.1 0.2 broadcast_in_dim.19
  199.3 3.1 %fusion.3 = bf16[1024,640]{1,0:T(8,128)(2,1)} fusion(s32[1024]{0:T(1024)S(1)} %sub.21, bf16[1024,128]{1,0:T(8,128)(2,1)S(1)} %broadcast_in_dim.19, bf16[1024,512]{1,0:T(8,128)(2,1)S(1)} %multiply_convert_fusion.1), kind=kOutput, calls=%fused_computation.11 | convolution fusion | flops 1346502656 | bytes 2625536 | tf_op jit(solution)/shard_map/dot_general | solution.py:471
  202.4 10.2 %all-to-all-start.1 = ((bf16[16,64,640]{2,1,0:T(8,128)(2,1)}), bf16[16,64,640]{2,1,0:T(8,128)(2,1)S(1)}, u32[]{:S(2)}, u32[]{:S(2)}) async-start(bf16[16,64,640]{2,1,0:T(8,128)(2,1)} %bitcast.12), calls=%async_computation.1 | async-start | bytes 2621440 | tf_op jit(solution)/shard_map/all_to_all | solution.py:470
  212.6 18.7 %all-to-all-done.1 = bf16[16,64,640]{2,1,0:T(8,128)(2,1)S(1)} async-done(((bf16[16,64,640]{2,1,0:T(8,128)(2,1)}), bf16[16,64,640]{2,1,0:T(8,128)(2,1)S(1)}, u32[]{:S(2)}, u32[]{:S(2)}) %all-to-all-start.1) | async-done | bytes 1310752 | tf_op jit(solution)/shard_map/all_to_all | solution.py:470
  231.2 0.2 multiply_reduce_fusion.2
  231.5 0.9 multiply_reduce_fusion
  232.4 9.0 %all_to_all.27 = f32[8,1,1024]{2,1,0:T(1,128)S(1)} all-to-all(f32[8,1,1024]{2,1,0:T(1,128)S(1)} %broadcast_in_dim.20), channel_id=1, replica_groups=mesh['teacher'=8,'student'=16] {'teacher'}, dimensions={0} | all-to-all | bytes 65536 | tf_op jit(solution)/shard_map/all_to_all | solution.py:445
  241.4 0.6 broadcast_in_dim.21
  242.0 5.4 %all-to-all-start.4 = ((f32[16,1,512]{2,1,0:T(1,128)}), f32[16,1,512]{2,1,0:T(1,128)S(1)}, u32[]{:S(2)}, u32[]{:S(2)}) async-start(f32[16,1,512]{2,1,0:T(1,128)} %broadcast_in_dim.21), calls=%async_computation.4 | async-start | bytes 65536 | tf_op jit(solution)/shard_map/all_to_all | solution.py:445
  247.4 6.2 %convolution_convert_fusion = bf16[2048,512]{1,0:T(8,128)(2,1)} fusion(bf16[1024,2048]{1,0:T(8,128)(2,1)} %get-tuple-element.7, f32[1024,512]{1,0:T(8,128)S(1)} %copy-done, f32[1024]{0:T(1024)S(1)} %broadcast_multiply_fusion, f32[1024]{0:T(1024)S(1)} %multiply_reduce_fusion.2, f32[512]{0:T(512)S(1)} %convert_element_type.32, f32[1024]{0:T(1024)S(1)} %bitcast.14, ...), kind=kOutput, calls=%fused_computation.3 | convolution fusion | flops 2153775104 | bytes 9451520 | tf_op jit(solution)/shard_map/dot_general | solution.py:485
  253.6 5.8 %all-to-all-start.3 = ((bf16[16,128,512]{2,1,0:T(8,128)(2,1)}), bf16[16,128,512]{2,1,0:T(8,128)(2,1)S(1)}, u32[]{:S(2)}, u32[]{:S(2)}) async-start(bf16[16,128,512]{2,1,0:T(8,128)(2,1)} %bitcast.11), calls=%async_computation.3 | async-start | bytes 4194304 | tf_op jit(solution)/shard_map/all_to_all | solution.py:489
  259.4 0.6 reduce_sum.79
  260.0 27.0 %all-to-all-done.3 = bf16[16,128,512]{2,1,0:T(8,128)(2,1)S(1)} async-done(((bf16[16,128,512]{2,1,0:T(8,128)(2,1)}), bf16[16,128,512]{2,1,0:T(8,128)(2,1)S(1)}, u32[]{:S(2)}, u32[]{:S(2)}) %all-to-all-start.3) | async-done | bytes 2097184 | tf_op jit(solution)/shard_map/all_to_all | solution.py:489
  287.0 1.0 convert_reduce_fusion
  (16 shorter events, 0.2 us)
Async XLA Ops:
  183.3 15.5 %copy-start.1 = (bf16[1024,512]{1,0:T(8,128)(2,1)S(1)}, bf16[1024,512]{1,0:T(8,128)(2,1)}, u32[]{:S(2)}) copy-start(bf16[1024,512]{1,0:T(8,128)(2,1)} %get-tuple-element.11) | copy-start | bytes 3145732
  186.6 12.2 %all-to-all-start = ((f32[8,2,1024]{2,1,0:T(2,128)}), f32[8,2,1024]{2,1,0:T(2,128)S(1)}, u32[]{:S(2)}, u32[]{:S(2)}) async-start(f32[8,2,1024]{2,1,0:T(2,128)} %broadcast_in_dim.16), calls=%async_computation | async-start | bytes 131072 | tf_op jit(solution)/shard_map/all_to_all | solution.py:445
  202.4 10.2 %copy-start.2 = (bf16[512]{0:T(512)(128)(2,1)S(1)}, bf16[512]{0:T(512)(128)(2,1)}, u32[]{:S(2)}) copy-start(bf16[512]{0:T(512)(128)(2,1)} %param.19) | copy-start | bytes 3076
  202.4 29.1 %copy-start = (f32[1024,512]{1,0:T(8,128)S(1)}, f32[1024,512]{1,0:T(8,128)}, u32[]{:S(2)}) copy-start(f32[1024,512]{1,0:T(8,128)} %get-tuple-element.10) | copy-start | bytes 6291460
  202.4 28.8 %all-to-all-start.1 = ((bf16[16,64,640]{2,1,0:T(8,128)(2,1)}), bf16[16,64,640]{2,1,0:T(8,128)(2,1)S(1)}, u32[]{:S(2)}, u32[]{:S(2)}) async-start(bf16[16,64,640]{2,1,0:T(8,128)(2,1)} %bitcast.12), calls=%async_computation.1 | async-start | bytes 2621440 | tf_op jit(solution)/shard_map/all_to_all | solution.py:470
  242.0 11.6 %all-to-all-start.4 = ((f32[16,1,512]{2,1,0:T(1,128)}), f32[16,1,512]{2,1,0:T(1,128)S(1)}, u32[]{:S(2)}, u32[]{:S(2)}) async-start(f32[16,1,512]{2,1,0:T(1,128)} %broadcast_in_dim.21), calls=%async_computation.4 | async-start | bytes 65536 | tf_op jit(solution)/shard_map/all_to_all | solution.py:445
  253.6 33.4 %all-to-all-start.3 = ((bf16[16,128,512]{2,1,0:T(8,128)(2,1)}), bf16[16,128,512]{2,1,0:T(8,128)(2,1)S(1)}, u32[]{:S(2)}, u32[]{:S(2)}) async-start(bf16[16,128,512]{2,1,0:T(8,128)(2,1)} %bitcast.11), calls=%async_computation.3 | async-start | bytes 4194304 | tf_op jit(solution)/shard_map/all_to_all | solution.py:489

commit v2 on v1

--- a/solution.py
+++ b/solution.py
@@ -14,7 +14,8 @@
 
 BF = jnp.bfloat16
 F32 = jnp.float32
-SLOTS = 160
+SLOTS = 256
+LOSS = 1.0 / math.sqrt(16384)
 
 
 def div(a, b):
@@ -86,20 +87,41 @@
         c.wait_recv()
 
 
-def gather_kernel(
-    tin, tattn, tw, tgain, proj, sin, sattn, su,
-    target_out, sq_out, sres_out, attn_out, ssq_out,
+def to_rows(lanes, out):
+    for q in range(8):
+        turned = jnp.transpose(lanes[q * 128 : q * 128 + 128, :])
+        out[q : q + 1, :] = jnp.sum(turned, axis=0, keepdims=True)
+
+
+def to_columns(rows, out):
+    for q in range(8):
+        wide = jnp.broadcast_to(rows[q : q + 1, :], (128, 128))
+        out[q * 128 : q * 128 + 128, :] = jnp.transpose(wide)
+
+
+def fold(a):
+    return a[:, 0:128] + a[:, 128:256] + a[:, 256:384] + a[:, 384:512]
+
+
+def step_kernel(
+    tin, tattn, tw, tgain, proj, sin, sattn, su, sgain, tokens, order,
+    weight_out, gain_out,
     bufA, bufC, bufW, bufP, bufU, tinv, sinv, hid,
     tmpA, tmpC, tmpE, r1, r2, r3, zs,
+    sq_out, sres_out, ssq_out, target, frecv, gn, sibr, grecv, tok, rowbuf,
+    tcol, scol, lcol, stage, exch, gstage, gains,
     send, recv, local,
 ):
     p = Place()
     up, down = {"dy": 1}, {"dy": -1}
     barrier = pltpu.get_barrier_semaphore()
-    near = [dict(dy=1), dict(dy=-1), dict(dz=1), dict(dz=-1), dict(dx=1), dict(dx=-1), dict(dc=1)]
-    for n in near:
-        pl.semaphore_signal(barrier, inc=1, device_id=p.dev(**n), device_id_type=pl.DeviceIdType.MESH)
-    pl.semaphore_wait(barrier, len(near))
+    teachers = [{"teacher": rem(p.t + j, 8), "student": p.s} for j in range(1, 8)]
+    students = [{"teacher": p.t, "student": rem(p.s + j, 16)} for j in range(1, 16)]
+    across = {"teacher": rem(p.t + 4, 8), "student": rem(p.s + 8, 16)}
+    met = teachers + students + [across]
+    for d in met:
+        pl.semaphore_signal(barrier, inc=1, device_id=d, device_id_type=pl.DeviceIdType.MESH)
+    pl.semaphore_wait(barrier, len(met))
     net = Net(send, recv)
 
     A = (tattn, bufA, tmpA, 512)
@@ -205,6 +227,8 @@
     bring(su, bufU.at[p.s])
     bring(sin, sinv)
     cown = t_own(C)
+    told = [net.copy(tokens, tok.at[p.s], d) for d in students]
+    bring(tokens, tok.at[p.s])
 
     ahop2 = t_hop2(A, ahop1)
     chop1 = t_hop1(C)
@@ -266,13 +290,17 @@
             acc = acc + jnp.dot(bufA[t, rows, :], w, preferred_element_type=F32)
         square = acc * acc
         sq_out[rows, :] += square[:, 0:128] + square[:, 128:256] + square[:, 256:384] + square[:, 384:512]
-        hid[rows, cols] = (acc * tgain[:, cols].astype(F32)).astype(BF)
+        hid[rows, cols] = (acc * tgain[:, cols]).astype(BF)
         return carry
 
     lax.fori_loop(0, 2, first, 0)
     cfwd2 = t_forward(C, *cpart, 2)
     lax.fori_loop(2, 4, first, 0)
-    net.sent([*aown[0], *aown[1], *ahop1, *ahop2, *afwd, *apart[0], *apart[1], *afwd2])
+    early = list(net.open)
+    a_sends = [*aown[0], *aown[1], *ahop1, *ahop2, *afwd, *apart[0], *apart[1], *afwd2]
+    net.sent(a_sends)
+    gone = {id(c) for c in a_sends}
+    early = [c for c in early if id(c) not in gone]
 
     def project(k):
         def step(i, carry):
@@ -337,17 +365,24 @@
     project(k_far)
     project(k_near)
 
+    def exchange(kind):
+        return [net.copy(stage.at[kind], exch.at[kind, p.t], d) for d in teachers]
+
+    def exchanged(kind, copies):
+        exch[kind, p.t] = stage[kind]
+        got(*copies)
+        total = exch[kind, 0]
+        for t in range(1, 8):
+            total = total + exch[kind, t]
+        return total
+
+    to_rows(sq_out, stage.at[0])
+    tsums = exchange(0)
+
     got(cown[0][1], cown[1][0], *cfwd, cpart[0][1], cpart[1][0], *cfwd2)
     got(*sfwd2["U"])
     ushared.append(share(U, s_index(2, True)))
     got(*ushared)
-    outs = []
-    for t in range(8):
-        c = pltpu.make_async_copy(
-            bufC.at[t], attn_out.at[:, pl.ds(t * 256, 256)], local.at[len(locals_) + t]
-        )
-        c.start()
-        outs.append(c)
 
     def student(i, carry):
         rows = pl.ds(pl.multiple_of(i * 512, 512), 512)
@@ -355,12 +390,56 @@
         for t in range(8):
             w = bufU[2 * t : 2 * t + 2].reshape(256, 512)
             acc = acc + jnp.dot(bufC[t, rows, :], w, preferred_element_type=F32)
-        square = acc * acc
-        ssq_out[rows, :] = square[:, 0:128] + square[:, 128:256] + square[:, 256:384] + square[:, 384:512]
+        ssq_out[rows, :] = fold(acc * acc)
         sres_out[rows, :] = acc
         return carry
 
     lax.fori_loop(0, 2, student, 0)
+    to_rows(ssq_out, stage.at[1])
+    ssums = exchange(1)
+
+    net.sent(early)
+
+    def turn(i, carry):
+        t = div(i, 8)
+        rows = pl.ds(pl.multiple_of(rem(i, 8) * 128, 128), 128)
+        block = bufC[t, rows, :].astype(F32)
+        at = pl.ds(pl.multiple_of(rem(t, 2) * 128, 128), 128)
+        for core in range(2):
+            turned = jnp.transpose(block[:, core * 128 : core * 128 + 128])
+            bufW[core * 4 + div(t, 2), at, rows] = turned.astype(BF)
+        return carry
+
+    lax.fori_loop(0, 64, turn, 0)
+
+    wide = lax.broadcasted_iota(jnp.int32, (64, 1024), 1).astype(F32)
+    narrow = lax.broadcasted_iota(jnp.int32, (64, 128), 1).astype(F32)
+    rowbuf[...] = jnp.zeros_like(rowbuf)
+    for m in range(16):
+        b = rem(p.s + m, 16)
+        rowbuf[0, m : m + 1, :] = order[pl.ds(b * 8 + div(p.s, 2), 1), :].astype(F32)
+    rowbuf[1, 0:8, :] = order[pl.ds(pl.multiple_of(p.s * 8, 8), 8), :].astype(F32)
+    for n in range(2):
+        rowbuf[2 + n] = jnp.transpose(rowbuf[n])
+    half = pl.ds(pl.multiple_of(rem(p.s, 2) * 64, 64), 64)
+    base = (p.s * 1024).astype(F32)
+    mine = rowbuf[2, half, :] - base
+    for m in range(16):
+        hid[m * 64 : m * 64 + 64, :] = jnp.where(wide == mine[:, m : m + 1], 1.0, 0.0).astype(BF)
+
+    got(*told)
+    for b in range(16):
+        low = (b % 2) * 64
+        named = rowbuf[3, low : low + 64, b // 2 : b // 2 + 1] - float(b * 1024)
+        live = jnp.where(tok[b] != PAD_ID, LOSS, 0.0)
+        acc = jnp.zeros((64, 128), F32)
+        for q in range(8):
+            acc = acc + jnp.where(narrow == named - float(q * 128), live[q : q + 1, :], 0.0)
+        total = jnp.sum(acc, axis=1, keepdims=True)
+        lcol[b * 64 : b * 64 + 64, :] = jnp.broadcast_to(total, (64, 128))
+
+    to_columns(lax.rsqrt(exchanged(0, tsums) / DT + epsilon), tcol)
+    to_columns(lax.rsqrt(exchanged(1, ssums) / DS + epsilon), scol)
 
     def three(n, k, base, i):
         at = pl.ds(pl.multiple_of(base + i * 128, 128), 128)
@@ -389,30 +468,99 @@
 
     def near_sum(i, carry):
         at, total = three(1, k_near, 0, i)
-        target_out[at, :] = (total + r3[at, :].astype(F32)).astype(BF)
+        total = total + r3[at, :].astype(F32)
+        target[at, :] = (total * tcol[at, 0:1]).astype(BF)
         return carry
 
     lax.fori_loop(0, 8, near_sum, 0)
-    for c in outs:
-        c.wait()
+
+    moved = {}
+    left, right = pl.ds(0, 512), pl.ds(512, 512)
+    for group in (1, 2, 3, 0):
+        picked = jnp.dot(
+            hid[group * 256 : group * 256 + 256, :], target[...], preferred_element_type=F32
+        ).astype(BF)
+        tinv[group * 256 : group * 256 + 256, 0:512] = picked
+        if group == 0:
+            frecv[p.s] = picked[0:64, :]
+        for m in range(max(group * 4, 1), group * 4 + 4):
+            moved[m] = net.copy(tinv.at[m * 64 : m * 64 + 64, left], frecv.at[p.s], students[m - 1])
+
+    gain_values = sgain[...]
+    partial = jnp.zeros((1, 512), F32)
+    for m in (0, *range(4, 16), 1, 2, 3):
+        if m:
+            got(moved[m])
+        b = rem(p.s + (16 - m), 16)
+        rows = pl.ds(pl.multiple_of(b * 64, 64), 64)
+        normed = sres_out[rows, :] * scol[rows, 0:1]
+        grad_out = (normed * gain_values - frecv[b].astype(F32)) * lcol[rows, 0:1]
+        partial = partial + jnp.sum(grad_out * normed, axis=0, keepdims=True)
+        grad_norm = grad_out * gain_values
+        gn[rows, :] = grad_norm
+        ssq_out[rows, :] = fold(grad_norm * normed)
+    to_rows(ssq_out, stage.at[2])
+    inner = exchange(2)
+    gstage[...] = partial
+    gained = [net.copy(gstage, gains.at[p.s], d) for d in students]
+    net.sent(hop1)
+    to_columns(exchanged(2, inner) / DS, sq_out)
+
+    def grad(i, carry):
+        rows = pl.ds(pl.multiple_of(i * 128, 128), 128)
+        scale = scol[rows, 0:1]
+        normed = sres_out[rows, :] * scale
+        zs[rows, :] = (scale * (gn[rows, :] - normed * sq_out[rows, 0:1])).astype(BF)
+        return carry
+
+    lax.fori_loop(0, 8, grad, 0)
+
+    def product(core, i):
+        return jnp.dot(bufW[core * 4 + i], zs[...], preferred_element_type=F32)
+
+    halves = []
+    for i in range(4):
+        sinv[i * 256 : i * 256 + 256, :] = product(1 - p.core, i).astype(BF)
+        part = pl.ds(i * 256, 256)
+        halves.append(net.copy(sinv.at[part, :], sibr.at[part, :], sib))
+    for i in range(4):
+        own_part = product(p.core, i)
+        got(halves[i])
+        total = own_part + sibr[i * 256 : i * 256 + 256, :].astype(F32)
+        tinv[i * 256 : i * 256 + 256, 512:1024] = total.astype(BF)
+    chip = div(p.s, 2)
+    parts = []
+    for m in range(1, 8):
+        q = rem(chip + m, 8)
+        rows = pl.ds(pl.multiple_of(q * 128, 128), 128)
+        to = {"teacher": p.t, "student": q * 2 + p.core}
+        parts.append(net.copy(tinv.at[rows, right], grecv.at[m - 1], to))
+    gains[p.s] = gstage[...]
+    got(*gained)
+    total_gain = gains[0]
+    for b in range(1, 16):
+        total_gain = total_gain + gains[b]
+    gain_out[...] = total_gain
+    total = tinv[pl.ds(pl.multiple_of(chip * 128, 128), 128), 512:1024].astype(F32)
+    for m in range(7):
+        got(parts[m])
+        total = total + grecv[m].astype(F32)
+    weight_out[...] = total
     net.finish()
 
 
-def gathered(tin, tattn, tw, tgain, proj, sin, sattn, su):
+def step(tin, tattn, tw, tgain, proj, sin, sattn, su, sgain, token_ids, row_order):
     anywhere = pl.BlockSpec(memory_space=pl.ANY)
     vmem = pl.BlockSpec(memory_space=pltpu.VMEM)
     V = pltpu.VMEM
-    return pl.pallas_call(
-        gather_kernel,
+    weight, gain = pl.pallas_call(
+        step_kernel,
         out_shape=(
-            jax.ShapeDtypeStruct((1024, 512), BF),
-            jax.ShapeDtypeStruct((1024, 128), F32),
-            jax.ShapeDtypeStruct((1024, 512), F32),
-            jax.ShapeDtypeStruct((1024, 2048), BF),
-            jax.ShapeDtypeStruct((1024, 128), F32),
+            jax.ShapeDtypeStruct((128, 512), F32),
+            jax.ShapeDtypeStruct((1, 512), F32),
         ),
-        in_specs=[anywhere, anywhere, anywhere, vmem, anywhere, anywhere, anywhere, anywhere],
-        out_specs=(vmem, vmem, vmem, anywhere, vmem),
+        in_specs=[anywhere] * 3 + [vmem] + [anywhere] * 4 + [vmem, anywhere, vmem],
+        out_specs=(vmem, vmem),
         scratch_shapes=[
             V((8, 1024, 512), BF),
             V((8, 1024, 256), BF),
@@ -429,6 +577,23 @@
             V((2, 2, 1024, 512), BF),
             V((1024, 512), BF),
             V((1024, 512), BF),
+            V((1024, 128), F32),
+            V((1024, 512), F32),
+            V((1024, 128), F32),
+            V((1024, 512), BF),
+            V((16, 64, 512), BF),
+            V((1024, 512), F32),
+            V((1024, 512), BF),
+            V((7, 128, 512), BF),
+            V((16, 8, 128), jnp.int32),
+            V((4, 128, 128), F32),
+            V((1024, 128), F32),
+            V((1024, 128), F32),
+            V((1024, 128), F32),
+            V((3, 8, 128), F32),
+            V((3, 8, 8, 128), F32),
+            V((1, 512), F32),
+            V((16, 1, 512), F32),
             pltpu.SemaphoreType.DMA((SLOTS,)),
             pltpu.SemaphoreType.DMA((SLOTS,)),
             pltpu.SemaphoreType.DMA((16,)),
@@ -436,60 +601,12 @@
         compiler_params=pltpu.CompilerParams(
             collective_id=0, has_side_effects=True, vmem_limit_bytes=67043328
         ),
-        name="gathered",
-    )(tin, tattn, tw, tgain.reshape(1, -1), proj, sin, sattn, su)
-
-
-def sent_to_all(array, axis):
-    peers = lax.axis_size(axis)
-    return lax.all_to_all(
-        jnp.broadcast_to(array[None], (peers, *array.shape)), axis, 0, 0, tiled=True
+        name="step",
+    )(
+        tin, tattn, tw, tgain.astype(F32).reshape(1, -1), proj, sin, sattn, su,
+        sgain.astype(F32).reshape(1, -1), token_ids.reshape(8, 128), row_order.reshape(128, 128),
     )
-
-
-def of_everyone(array, axis):
-    return jnp.sum(sent_to_all(array, axis), axis=0)
-
-
-def shards(tin, tattn, tw, tgain, proj, sin, sattn, su, sgain, token_ids, row_order):
-    s = lax.axis_index("student")
-    row_count = 1024
-    target_raw, sq, student_res, attn_student, ssq = gathered(
-        tin, tattn, tw, tgain, proj, sin, sattn, su
-    )
-    sums = of_everyone(jnp.stack([jnp.sum(sq, axis=1), jnp.sum(ssq, axis=1)]), "teacher")
-    teacher_scale = lax.rsqrt(sums[0] / DT + epsilon)
-    student_scale = lax.rsqrt(sums[1] / DS + epsilon)
-    target_rows = (target_raw.astype(F32) * teacher_scale[:, None]).astype(BF)
-    local_rows = lax.dynamic_index_in_dim(
-        row_order.reshape(16, 16, 64), s, 1, keepdims=False
-    ).reshape(1024) - s * row_count
-    pick = (local_rows[:, None] == jnp.arange(1024)[None, :]).astype(BF)
-    live_rows = jnp.where(token_ids != PAD_ID, 1.0, 0.0).astype(BF)
-    both = jnp.concatenate([target_rows, jnp.broadcast_to(live_rows[:, None], (1024, 128))], axis=1)
-    moved = lax.all_to_all(
-        jnp.dot(pick, both, preferred_element_type=F32).astype(BF).reshape(16, 64, 640),
-        "student", 0, 0, tiled=True,
-    ).reshape(1024, 640)
-    target = moved[:, :512].astype(F32)
-    weight_mask = moved[:, 512].astype(F32)
-    normed = student_res * student_scale[:, None]
-    gain_values = sgain.astype(F32)[None, :]
-    distance = normed * gain_values - target
-    loss_weight = 1.0 / math.sqrt(16384)
-    grad_out = distance * (weight_mask * loss_weight)[:, None]
-    gain_part = jnp.sum(grad_out * normed, axis=0)
-    grad_norm = grad_out * gain_values
-    inner_sum = of_everyone(jnp.sum(grad_norm * normed, axis=1), "teacher")
-    grad_res = (student_scale[:, None] * (grad_norm - normed * (inner_sum / DS)[:, None])).astype(BF)
-    parts = lax.dot_general(
-        attn_student, grad_res, (((0,), (0,)), ((), ())), preferred_element_type=F32
-    ).astype(BF)
-    grad_weight = jnp.sum(
-        lax.all_to_all(parts.reshape(16, 128, 512), "student", 0, 0, tiled=True).astype(F32), axis=0
-    )
-    grad_gain = of_everyone(gain_part, "student")
-    return (grad_weight, grad_gain)
+    return weight, gain.reshape(512)
 
 
 def solution(mesh):
@@ -507,7 +624,7 @@
         P(),
     )
     return jax.shard_map(
-        shards,
+        step,
         mesh=mesh,
         in_specs=placed,
         out_specs=(P("student", "teacher"), P("teacher")),

time: 289 us -> 260 us (0.90)
  Pallas kernels: 181 us -> 254 us
  waiting for transfers between devices: 50.6 us -> 0 us
  starting transfers between devices: 26.8 us -> 0 us
  matrix products: 9.23 us -> 0 us
  blocking collectives: 8.99 us -> 0 us
  other arithmetic: 6.43 us -> 2.53 us
    pallas_call x1, Pallas kernels: 181 us -> 254 us  [step(): pl.pallas_call(step_kernel, out_shape=(jax.ShapeDtypeStruct((128, 512), F...]
    all_to_all x4 -> x0, waiting for transfers between devices: 50.6 us -> none  [the longest x1 27 us: shards(): lax.all_to_all(parts.reshape(16, 128, 512), 'student', 0, 0, tiled=True)]
    all_to_all x4 -> x0, starting transfers between devices: 26.8 us -> none  [the longest x2 10.8 us: sent_to_all(): lax.all_to_all(jnp.broadcast_to(array[None], (peers, *array.shape)), axis...]
    dot_general x2 -> x0, matrix products: 9.23 us -> none  [the longest x1 6.17 us: shards(): lax.dot_general(attn_student, grad_res, (((0,), (0,)), ((), ())), preferr...]
    all_to_all x1 -> x0, blocking collectives: 8.99 us -> none  [sent_to_all(): lax.all_to_all(jnp.broadcast_to(array[None], (peers, *array.shape)), axis...]
    reduce_sum x7 -> x0, other arithmetic: 5.17 us -> none  [the longest x1 1.34 us: shards(): jnp.sum(sq, axis=1)]
    unnamed x6 -> x2, local copies, waits for them, and re-layouts: 0.01 us -> 2.92 us
  transfers between devices with their start and end apart: 4 -> 0, of which waited for: 3 -> 0; matrix products, arithmetic and copies ran while one was open for 3% -> 0% of each run, Pallas kernels for 0% -> 0%
where the time goes in v2:
time: 260 us
  Pallas kernels  254 us (98%)
  local copies, waits for them, and re-layouts  2.92 us (1%)
    pallas_call x1, Pallas kernels, step(): pl.pallas_call(step_kernel, out_shape=(jax.ShapeDtypeStruct((128, 512), F...  254 us

profile of v2, /device:TPU:1, one launch (start us, length us, event | category | flops | bytes accessed | tf_op | source)
XLA Modules:
  0.0 260.0 jit_solution(7439291413169763844)
XLA Ops:
  0.6 1.3 reshape.32
  1.9 1.3 reshape.30
  3.2 253.9 %step.1 = (f32[128,512]{1,0:T(8,128)}, f32[1,512]{1,0:T(1,128)}) custom-call(bf16[1024,1024]{1,0:T(8,128)(2,1)} %tin.1, bf16[1024,512]{1,0:T(8,128)(2,1)} %tattn.1, bf16[256,1024]{1,0:T(8,128)(2,1)} %tw.1, f32[1,1024]{1,0:T(1,128)} %bitcast.6, bf16[1024,256]{1,0:T(8,128)(2,1)} %proj.1, bf16[1024,512]{1,0:T(8,128)(2,1)} %sin.1, bf16[1024,256]{1,0:T(8,128)(2,1)} %sattn.1, ...), custom_call_target="tpu_custom_call" | custom-call | tf_op jit(solution)/shard_map/step/pallas_call | solution.py:556
  257.1 1.7 copy.15
  258.7 1.2 copy.16

commit v3 on v2

--- a/solution.py
+++ b/solution.py
@@ -107,9 +107,9 @@
     tin, tattn, tw, tgain, proj, sin, sattn, su, sgain, tokens, order,
     weight_out, gain_out,
     bufA, bufC, bufW, bufP, bufU, tinv, sinv, hid,
-    tmpA, tmpC, tmpE, r1, r2, r3, zs,
+    pick, tmpA, tmpC, tmpD, tmpE, tmpZ, rz, r1, r2, b1, b2, r3, zs,
     sq_out, sres_out, ssq_out, target, frecv, gn, sibr, grecv, tok, rowbuf,
-    tcol, scol, lcol, stage, exch, gstage, gains,
+    scol, lcol, stage, exch, gstage, gains,
     send, recv, local,
 ):
     p = Place()
@@ -124,19 +124,20 @@
     pl.semaphore_wait(barrier, len(met))
     net = Net(send, recv)
 
-    A = (tattn, bufA, tmpA, 512)
-    C = (sattn, bufC, tmpC, 512)
-    W = (tw, bufW, 128)
-    Q = (proj, bufP, 512)
-    U = (su, bufU, 64)
+    A = (tattn, bufA, tmpA, pl.ds(0, 512), 512)
+    C = (sattn, bufC, tmpC, pl.ds(0, 128), 512)
+    D = (sattn, bufC, tmpD, pl.ds(128, 128), 512)
+    W = (tw, bufW, None, pl.ds(0, 1024), 128)
+    Q = (proj, bufP, None, pl.ds(0, 256), 512)
+    U = (su, bufU, None, pl.ds(0, 512), 64)
 
     def own(arr, h):
         half = arr[-1]
-        return arr[0].at[pl.ds(h * half, half), :]
+        return arr[0].at[pl.ds(h * half, half), arr[3]]
 
     def slot(arr, i, h):
         half = arr[-1]
-        return arr[1].at[i, pl.ds(h * half, half), :]
+        return arr[1].at[i, pl.ds(h * half, half), arr[3]]
 
     tp = p.index(dz=2)[0]
     zpart = {"teacher": p.t, "student": rem(p.s + 8, 16)}
@@ -181,6 +182,21 @@
         ups = [net.copy(slot(arr, tp, h), slot(arr, tp, h), p.dev(dy=1)) for h in (0, 1)]
         downs = [net.copy(slot(arr, tp, h), slot(arr, tp, h), p.dev(dy=-1)) for h in (1, 0)][::-1]
         return ups, downs
+
+    def d_hop1(dy, halves=(0, 1)):
+        out = []
+        for h in halves:
+            src = own(D, h) if dy == 0 else slot(D, p.index(dy=dy)[0], h)
+            out.append(net.copy(src, tmpD.at[dy % 4, h], p.dev(dz=(1, -1)[h])))
+        return out
+
+    def d_hop2(dy, hop1):
+        out = []
+        for h, c in enumerate(hop1):
+            got(c)
+            at = slot(D, p.index(dz=(-1, 1)[h], dy=dy)[0], h)
+            out.append(net.copy(tmpD.at[dy % 4, h], at, p.dev(dz=(1, -1)[h])))
+        return out
 
     def s_own(arr):
         ups = [net.copy(own(arr, h), slot(arr, p.s, h), p.dev(dx=1)) for h in (0, 1)]
@@ -226,24 +242,29 @@
     bring(sattn, bufC.at[p.t])
     bring(su, bufU.at[p.s])
     bring(sin, sinv)
-    cown = t_own(C)
+    down_ = t_own(D)
     told = [net.copy(tokens, tok.at[p.s], d) for d in students]
     bring(tokens, tok.at[p.s])
-
-    ahop2 = t_hop2(A, ahop1)
-    chop1 = t_hop1(C)
     sowns["U"] = s_own(U)
     ssides["U"] = s_side(U)
     shared.append(net.copy(U[0], U[1].at[p.s], sib))
     S = (("W", W), ("Q", Q), ("U", U))
     sfwd, sfwd2, sparts = {}, {}, {}
+
+    ahop2 = t_hop2(A, ahop1)
+    dhop1, dhop2 = {}, {}
+    dhop1[0] = d_hop1(0)
     for n, arr in S[:2]:
         sfwd[n] = s_forward(arr, *sowns[n], False)
     afwd = t_forward(A, *aown, 0)
-    for n, arr in S[:2]:
-        sparts[n] = s_partner(arr, ssides[n])
+    sparts["W"] = s_partner(W, ssides["W"])
+    dhop2[0] = d_hop2(0, dhop1[0])
+    sparts["Q"] = s_partner(Q, ssides["Q"])
     apart = t_partner(A, ahop2)
-    chop2 = t_hop2(C, chop1)
+    dfwd = t_forward(D, *down_, 0)
+    got(down_[0][1], down_[1][0])
+    dhop1[-1] = d_hop1(-1)
+    dhop1[1] = d_hop1(1)
     for n, arr in S[:2]:
         got(sowns[n][0][1], sowns[n][1][0])
         shared.append(share(arr, sp))
@@ -251,20 +272,23 @@
         shared.append(share(arr, s_index(1, False)))
     sfwd["U"] = s_forward(U, *sowns["U"], False)
     sparts["U"] = s_partner(U, ssides["U"])
+    dhop2[-1] = d_hop2(-1, dhop1[-1])
+    dhop2[1] = d_hop2(1, dhop1[1])
     for n, arr in S[:2]:
         sfwd2[n] = s_forward(arr, *sparts[n], True)
     afwd2 = t_forward(A, *apart, 2)
-    cfwd = t_forward(C, *cown, 0)
-    cpart = t_partner(C, chop2)
+    chop1 = t_hop1(C)
+    got(*dfwd)
+    dhop1[2] = d_hop1(2)
+    cown = t_own(C)
+    chop2 = t_hop2(C, chop1)
+    dhop2[2] = d_hop2(2, dhop1[2])
     for n, arr in S[:2]:
         got(*sfwd[n], sparts[n][0][1], sparts[n][1][0])
         shared.append(share(arr, s_index(2, False)))
         shared.append(share(arr, s_index(-1, True)))
         shared.append(share(arr, s_index(1, True)))
     sfwd2["U"] = s_forward(U, *sparts["U"], True)
-    for n, arr in S[:2]:
-        got(*sfwd2[n])
-        shared.append(share(arr, s_index(2, True)))
     got(sowns["U"][0][1], sowns["U"][1][0], sparts["U"][0][1], sparts["U"][1][0], *sfwd["U"])
     ushared = [
         share(U, sp),
@@ -274,143 +298,8 @@
         share(U, s_index(-1, True)),
         share(U, s_index(1, True)),
     ]
-    got(aown[0][1], aown[1][0], *afwd, apart[0][1], apart[1][0], *afwd2)
-    got(*shared)
     for c in locals_:
         c.wait()
-
-    sq_out[...] = jnp.zeros_like(sq_out)
-
-    def first(i, carry):
-        rows = pl.ds(pl.multiple_of(div(i, 2) * 512, 512), 512)
-        cols = pl.ds(pl.multiple_of(rem(i, 2) * 512, 512), 512)
-        acc = tinv[rows, cols].astype(F32)
-        for t in range(8):
-            w = bufW[2 * t : 2 * t + 2, :, cols].reshape(512, 512)
-            acc = acc + jnp.dot(bufA[t, rows, :], w, preferred_element_type=F32)
-        square = acc * acc
-        sq_out[rows, :] += square[:, 0:128] + square[:, 128:256] + square[:, 256:384] + square[:, 384:512]
-        hid[rows, cols] = (acc * tgain[:, cols]).astype(BF)
-        return carry
-
-    lax.fori_loop(0, 2, first, 0)
-    cfwd2 = t_forward(C, *cpart, 2)
-    lax.fori_loop(2, 4, first, 0)
-    early = list(net.open)
-    a_sends = [*aown[0], *aown[1], *ahop1, *ahop2, *afwd, *apart[0], *apart[1], *afwd2]
-    net.sent(a_sends)
-    gone = {id(c) for c in a_sends}
-    early = [c for c in early if id(c) not in gone]
-
-    def project(k):
-        def step(i, carry):
-            rows = pl.ds(pl.multiple_of(i * 512, 512), 512)
-            h = hid[rows, :]
-            bufA[k, rows, 0:256] = jnp.dot(h, bufP[2 * k], preferred_element_type=F32).astype(BF)
-            bufA[k, rows, 256:512] = jnp.dot(h, bufP[2 * k + 1], preferred_element_type=F32).astype(BF)
-            return carry
-
-        lax.fori_loop(0, 2, step, 0)
-
-    def block(far, dy):
-        zh = 1 - p.zh if far else p.zh
-        y = rem(p.y + (dy % 4), 4)
-        return zh * 4 + y
-
-    lo, hi = pl.ds(0, 512), pl.ds(512, 512)
-
-    def opening(n, far):
-        k = block(far, 2)
-        project(k)
-        return (
-            net.copy(bufA.at[k, lo, :], r1.at[n, 0], p.dev(dy=1)),
-            net.copy(bufA.at[k, hi, :], r1.at[n, 1], p.dev(dy=-1)),
-        )
-
-    def plain(n, far):
-        ku, kd = block(far, 1), block(far, -1)
-        project(ku)
-        u = net.copy(bufA.at[ku, hi, :], r2.at[n, 0, hi, :], p.dev(dy=1))
-        project(kd)
-        d = net.copy(bufA.at[kd, lo, :], r2.at[n, 1, lo, :], p.dev(dy=-1))
-        return u, d
-
-    def added(n, far, opened):
-        ku, kd = block(far, 1), block(far, -1)
-
-        def add(k, base, j):
-            def step(i, carry):
-                at = pl.ds(pl.multiple_of(i * 128, 128), 128)
-                rows = pl.ds(pl.multiple_of(base + i * 128, 128), 128)
-                bufA[k, rows, :] = (bufA[k, rows, :].astype(F32) + r1[n, j, at, :].astype(F32)).astype(BF)
-                return carry
-
-            lax.fori_loop(0, 4, step, 0)
-
-        got(opened[0])
-        add(ku, 0, 0)
-        u = net.copy(bufA.at[ku, lo, :], r2.at[n, 0, lo, :], p.dev(dy=1))
-        got(opened[1])
-        add(kd, 512, 1)
-        d = net.copy(bufA.at[kd, hi, :], r2.at[n, 1, hi, :], p.dev(dy=-1))
-        return u, d
-
-    open_far = opening(0, True)
-    plain_far = plain(0, True)
-    open_near = opening(1, False)
-    added_far = added(0, True, open_far)
-    plain_near = plain(1, False)
-    added_near = added(1, False, open_near)
-    k_far, k_near = block(True, 0), block(False, 0)
-    project(k_far)
-    project(k_near)
-
-    def exchange(kind):
-        return [net.copy(stage.at[kind], exch.at[kind, p.t], d) for d in teachers]
-
-    def exchanged(kind, copies):
-        exch[kind, p.t] = stage[kind]
-        got(*copies)
-        total = exch[kind, 0]
-        for t in range(1, 8):
-            total = total + exch[kind, t]
-        return total
-
-    to_rows(sq_out, stage.at[0])
-    tsums = exchange(0)
-
-    got(cown[0][1], cown[1][0], *cfwd, cpart[0][1], cpart[1][0], *cfwd2)
-    got(*sfwd2["U"])
-    ushared.append(share(U, s_index(2, True)))
-    got(*ushared)
-
-    def student(i, carry):
-        rows = pl.ds(pl.multiple_of(i * 512, 512), 512)
-        acc = sinv[rows, :].astype(F32)
-        for t in range(8):
-            w = bufU[2 * t : 2 * t + 2].reshape(256, 512)
-            acc = acc + jnp.dot(bufC[t, rows, :], w, preferred_element_type=F32)
-        ssq_out[rows, :] = fold(acc * acc)
-        sres_out[rows, :] = acc
-        return carry
-
-    lax.fori_loop(0, 2, student, 0)
-    to_rows(ssq_out, stage.at[1])
-    ssums = exchange(1)
-
-    net.sent(early)
-
-    def turn(i, carry):
-        t = div(i, 8)
-        rows = pl.ds(pl.multiple_of(rem(i, 8) * 128, 128), 128)
-        block = bufC[t, rows, :].astype(F32)
-        at = pl.ds(pl.multiple_of(rem(t, 2) * 128, 128), 128)
-        for core in range(2):
-            turned = jnp.transpose(block[:, core * 128 : core * 128 + 128])
-            bufW[core * 4 + div(t, 2), at, rows] = turned.astype(BF)
-        return carry
-
-    lax.fori_loop(0, 64, turn, 0)
 
     wide = lax.broadcasted_iota(jnp.int32, (64, 1024), 1).astype(F32)
     narrow = lax.broadcasted_iota(jnp.int32, (64, 128), 1).astype(F32)
@@ -425,7 +314,7 @@
     base = (p.s * 1024).astype(F32)
     mine = rowbuf[2, half, :] - base
     for m in range(16):
-        hid[m * 64 : m * 64 + 64, :] = jnp.where(wide == mine[:, m : m + 1], 1.0, 0.0).astype(BF)
+        pick[m * 64 : m * 64 + 64, :] = jnp.where(wide == mine[:, m : m + 1], 1.0, 0.0).astype(BF)
 
     got(*told)
     for b in range(16):
@@ -438,70 +327,284 @@
         total = jnp.sum(acc, axis=1, keepdims=True)
         lcol[b * 64 : b * 64 + 64, :] = jnp.broadcast_to(total, (64, 128))
 
-    to_columns(lax.rsqrt(exchanged(0, tsums) / DT + epsilon), tcol)
-    to_columns(lax.rsqrt(exchanged(1, ssums) / DS + epsilon), scol)
-
-    def three(n, k, base, i):
-        at = pl.ds(pl.multiple_of(base + i * 128, 128), 128)
-        return at, (
-            bufA[k, at, :].astype(F32) + r2[n, 0, at, :].astype(F32) + r2[n, 1, at, :].astype(F32)
+    for n, arr in S[:2]:
+        got(*sfwd2[n])
+        shared.append(share(arr, s_index(2, True)))
+    got(aown[0][1], aown[1][0], *afwd, apart[0][1], apart[1][0], *afwd2)
+    cfwd = t_forward(C, *cown, 0)
+    cpart = t_partner(C, chop2)
+    got(*shared)
+    sq_out[...] = jnp.zeros_like(sq_out)
+
+    def first(i, carry):
+        rows = pl.ds(pl.multiple_of(div(i, 2) * 512, 512), 512)
+        cols = pl.ds(pl.multiple_of(rem(i, 2) * 512, 512), 512)
+        acc = tinv[rows, cols].astype(F32)
+        for t in range(8):
+            w = bufW[2 * t : 2 * t + 2, :, cols].reshape(512, 512)
+            acc = acc + jnp.dot(bufA[t, rows, :], w, preferred_element_type=F32)
+        square = acc * acc
+        sq_out[rows, :] += square[:, 0:128] + square[:, 128:256] + square[:, 256:384] + square[:, 384:512]
+        hid[rows, cols] = (acc * tgain[:, cols]).astype(BF)
+        return carry
+
+    lax.fori_loop(0, 2, first, 0)
+    cfwd2 = t_forward(C, *cpart, 2)
+    lax.fori_loop(2, 4, first, 0)
+    early = list(net.open)
+    a_sends = [*aown[0], *aown[1], *ahop1, *ahop2, *afwd, *apart[0], *apart[1], *afwd2]
+    net.sent(a_sends)
+    gone = {id(c) for c in a_sends}
+    early = [c for c in early if id(c) not in gone]
+
+    def columns(half):
+        return pl.ds(half * 256, 256)
+
+    def project(k, half):
+        def step(i, carry):
+            rows = pl.ds(pl.multiple_of(i * 512, 512), 512)
+            bufA[k, rows, columns(half)] = jnp.dot(
+                hid[rows, :], bufP[2 * k + half], preferred_element_type=F32
+            ).astype(BF)
+            return carry
+
+        lax.fori_loop(0, 2, step, 0)
+
+    def block(far, dy):
+        zh = 1 - p.zh if far else p.zh
+        y = rem(p.y + (dy % 4), 4)
+        return zh * 4 + y
+
+    lo, hi = pl.ds(0, 512), pl.ds(512, 512)
+    right = pl.ds(512, 512)
+
+    def add(k, half, base, count, ref, rebase):
+        def step(i, carry):
+            at = pl.ds(pl.multiple_of(rebase + i * 128, 128), 128)
+            rows = pl.ds(pl.multiple_of(base + i * 128, 128), 128)
+            both = bufA[k, rows, columns(half)].astype(F32) + ref[at, :].astype(F32)
+            bufA[k, rows, columns(half)] = both.astype(BF)
+            return carry
+
+        lax.fori_loop(0, count, step, 0)
+
+    def piece(k, half, rows):
+        return bufA.at[k, rows, columns(half)]
+
+    def open_to(k, half, dst):
+        return (
+            net.copy(piece(k, half, lo), dst.at[0], p.dev(dy=1)),
+            net.copy(piece(k, half, hi), dst.at[1], p.dev(dy=-1)),
         )
 
-    got(*plain_far, *added_far)
+    def added(far, half, opened, src, dst):
+        ku, kd = block(far, 1), block(far, -1)
+        got(opened[0])
+        add(ku, half, 0, 4, src.at[0], 0)
+        u = net.copy(piece(ku, half, lo), dst.at[0, lo, :], p.dev(dy=1))
+        got(opened[1])
+        add(kd, half, 512, 4, src.at[1], 0)
+        d = net.copy(piece(kd, half, hi), dst.at[1, hi, :], p.dev(dy=-1))
+        return u, d
+
+    def plain_up(far, half, dst):
+        return net.copy(piece(block(far, 1), half, hi), dst.at[0, hi, :], p.dev(dy=1))
+
+    def plain_down(far, half, dst):
+        return net.copy(piece(block(far, -1), half, lo), dst.at[1, lo, :], p.dev(dy=-1))
+
+    z1, z2 = {}, {}
+
+    def z_first(dy):
+        k = block(True, dy)
+        project(k, 1)
+        z1[dy] = (
+            net.copy(piece(k, 1, lo), tmpZ.at[dy % 4, 0], p.dev(dz=1)),
+            net.copy(piece(k, 1, hi), tmpZ.at[dy % 4, 1], p.dev(dz=-1)),
+        )
+
+    def z_on(dy):
+        got(z1[dy][0])
+        a = net.copy(tmpZ.at[dy % 4, 0], rz.at[dy % 4, lo, :], p.dev(dz=1))
+        got(z1[dy][1])
+        b = net.copy(tmpZ.at[dy % 4, 1], rz.at[dy % 4, hi, :], p.dev(dz=-1))
+        z2[dy] = (a, b)
+
+    def z_add(dy):
+        got(*z2[dy])
+        add(block(False, dy), 1, 0, 8, rz.at[dy % 4], 0)
+
+    def exchange(kind):
+        return [net.copy(stage.at[kind], exch.at[kind, p.t], d) for d in teachers]
+
+    def exchanged(kind, copies):
+        exch[kind, p.t] = stage[kind]
+        got(*copies)
+        total = exch[kind, 0]
+        for t in range(1, 8):
+            total = total + exch[kind, t]
+        return total
+
+    z_first(2)
+    project(block(True, 2), 0)
+    open_far = open_to(block(True, 2), 0, r1.at[0])
+    z_first(1)
+    project(block(True, 1), 0)
+    up_far = plain_up(True, 0, r2.at[0])
+    project(block(True, -1), 0)
+    down_far = plain_down(True, 0, r2.at[0])
+    project(block(False, 2), 0)
+    open_near = open_to(block(False, 2), 0, r1.at[1])
+    z_on(2)
+    z_first(-1)
+    added_far = added(True, 0, open_far, r1.at[0], r2.at[0])
+    z_on(1)
+    z_first(0)
+    project(block(False, 1), 0)
+    up_near = plain_up(False, 0, r2.at[1])
+    project(block(False, -1), 0)
+    down_near = plain_down(False, 0, r2.at[1])
+    for dy in (2, 1, -1, 0):
+        project(block(False, dy), 1)
+    k_far, k_near = block(True, 0), block(False, 0)
+    project(k_far, 0)
+    project(k_near, 0)
+    got(cown[0][1], cown[1][0], *cfwd, cpart[0][1], cpart[1][0], *cfwd2)
+    got(*dhop2[0], *dhop2[1], *dhop2[-1], *dhop2[2])
+    got(*sfwd2["U"])
+    ushared.append(share(U, s_index(2, True)))
+    got(*ushared)
+
+    def student(i, carry):
+        rows = pl.ds(pl.multiple_of(i * 512, 512), 512)
+        acc = sinv[rows, :].astype(F32)
+        for t in range(8):
+            w = bufU[2 * t : 2 * t + 2].reshape(256, 512)
+            acc = acc + jnp.dot(bufC[t, rows, :], w, preferred_element_type=F32)
+        ssq_out[rows, :] = fold(acc * acc)
+        sres_out[rows, :] = acc
+        return carry
+
+    lax.fori_loop(0, 2, student, 0)
+    to_rows(ssq_out, stage.at[1])
+    ssums = exchange(1)
+
+    net.sent(early)
+
+    def turn(i, carry):
+        t = div(i, 8)
+        rows = pl.ds(pl.multiple_of(rem(i, 8) * 128, 128), 128)
+        block = bufC[t, rows, :].astype(F32)
+        at = pl.ds(pl.multiple_of(rem(t, 2) * 128, 128), 128)
+        for core in range(2):
+            turned = jnp.transpose(block[:, core * 128 : core * 128 + 128])
+            bufW[core * 4 + div(t, 2), at, rows] = turned.astype(BF)
+        return carry
+
+    z_on(-1)
+    z_add(2)
+    opened = open_to(block(False, 2), 1, b1)
+    added_near = added(False, 0, open_near, r1.at[1], r2.at[1])
+    lax.fori_loop(0, 16, turn, 0)
+
+    def three(k, half, src, i):
+        at = pl.ds(pl.multiple_of(i * 128, 128), 128)
+        own_part = bufA[k, at, columns(half)].astype(F32)
+        return at, own_part + src[0, at, :].astype(F32) + src[1, at, :].astype(F32)
+
+    got(up_far, down_far, *added_far)
 
     def far_sum(i, carry):
-        at, total = three(0, k_far, 0, i)
-        zs[at, :] = total.astype(BF)
+        at, total = three(k_far, 0, r2.at[0], i)
+        zs[at, columns(0)] = total.astype(BF)
         return carry
 
     lax.fori_loop(0, 8, far_sum, 0)
     hop1 = (
-        net.copy(zs.at[lo, :], tmpE.at[0], p.dev(dz=1)),
-        net.copy(zs.at[hi, :], tmpE.at[1], p.dev(dz=-1)),
+        net.copy(zs.at[lo, columns(0)], tmpE.at[0], p.dev(dz=1)),
+        net.copy(zs.at[hi, columns(0)], tmpE.at[1], p.dev(dz=-1)),
     )
+    z_add(1)
+    up_last = plain_up(False, 1, b2)
+    z_on(0)
+    to_rows(sq_out, stage.at[0])
+    tsums = exchange(0)
+    lax.fori_loop(16, 32, turn, 0)
     got(hop1[0])
     h2a = net.copy(tmpE.at[0], r3.at[lo, :], p.dev(dz=1))
     got(hop1[1])
     h2b = net.copy(tmpE.at[1], r3.at[hi, :], p.dev(dz=-1))
-    got(*plain_near, *added_near)
+    z_add(-1)
+    down_last = plain_down(False, 1, b2)
+    added_last = added(False, 1, opened, b1, b2)
+    lax.fori_loop(32, 48, turn, 0)
+    to_columns(lax.rsqrt(exchanged(0, tsums) / DT + epsilon), sq_out)
+    to_columns(lax.rsqrt(exchanged(1, ssums) / DS + epsilon), scol)
+    got(up_near, down_near, *added_near)
+    lax.fori_loop(48, 64, turn, 0)
     got(h2a, h2b)
 
     def near_sum(i, carry):
-        at, total = three(1, k_near, 0, i)
+        at, total = three(k_near, 0, r2.at[1], i)
         total = total + r3[at, :].astype(F32)
-        target[at, :] = (total * tcol[at, 0:1]).astype(BF)
+        target[at, columns(0)] = (total * sq_out[at, 0:1]).astype(BF)
         return carry
 
     lax.fori_loop(0, 8, near_sum, 0)
 
-    moved = {}
-    left, right = pl.ds(0, 512), pl.ds(512, 512)
-    for group in (1, 2, 3, 0):
-        picked = jnp.dot(
-            hid[group * 256 : group * 256 + 256, :], target[...], preferred_element_type=F32
-        ).astype(BF)
-        tinv[group * 256 : group * 256 + 256, 0:512] = picked
-        if group == 0:
-            frecv[p.s] = picked[0:64, :]
-        for m in range(max(group * 4, 1), group * 4 + 4):
-            moved[m] = net.copy(tinv.at[m * 64 : m * 64 + 64, left], frecv.at[p.s], students[m - 1])
-
-    gain_values = sgain[...]
-    partial = jnp.zeros((1, 512), F32)
-    for m in (0, *range(4, 16), 1, 2, 3):
-        if m:
-            got(moved[m])
-        b = rem(p.s + (16 - m), 16)
-        rows = pl.ds(pl.multiple_of(b * 64, 64), 64)
-        normed = sres_out[rows, :] * scol[rows, 0:1]
-        grad_out = (normed * gain_values - frecv[b].astype(F32)) * lcol[rows, 0:1]
-        partial = partial + jnp.sum(grad_out * normed, axis=0, keepdims=True)
-        grad_norm = grad_out * gain_values
-        gn[rows, :] = grad_norm
-        ssq_out[rows, :] = fold(grad_norm * normed)
+    def send_rows(half):
+        out = {}
+        for group in (1, 2, 3, 0):
+            rows = slice(group * 256, group * 256 + 256)
+            picked = jnp.dot(
+                pick[rows, :], target[:, columns(half)], preferred_element_type=F32
+            ).astype(BF)
+            tinv[rows, columns(half)] = picked
+            if group == 0:
+                frecv[p.s, :, columns(half)] = picked[0:64, :]
+            for m in range(max(group * 4, 1), group * 4 + 4):
+                out[m] = net.copy(
+                    tinv.at[pl.ds(m * 64, 64), columns(half)],
+                    frecv.at[p.s, :, columns(half)],
+                    students[m - 1],
+                )
+        return out
+
+    moved = send_rows(0)
+    z_add(0)
+    got(up_last, down_last, *added_last)
+
+    def last_sum(i, carry):
+        at, total = three(k_near, 1, b2, i)
+        target[at, columns(1)] = (total * sq_out[at, 0:1]).astype(BF)
+        return carry
+
+    lax.fori_loop(0, 8, last_sum, 0)
+    moved_last = send_rows(1)
+
+    def compared(half, copies):
+        cols = columns(half)
+        gain_values = sgain[:, cols]
+        partial = jnp.zeros((1, 256), F32)
+        for m in (0, *range(4, 16), 1, 2, 3):
+            if m:
+                got(copies[m])
+            b = rem(p.s + (16 - m), 16)
+            rows = pl.ds(pl.multiple_of(b * 64, 64), 64)
+            normed = sres_out[rows, cols] * scol[rows, 0:1]
+            grad_out = (normed * gain_values - frecv[b, :, cols].astype(F32)) * lcol[rows, 0:1]
+            partial = partial + jnp.sum(grad_out * normed, axis=0, keepdims=True)
+            grad_norm = grad_out * gain_values
+            gn[rows, cols] = grad_norm
+            product = grad_norm * normed
+            lanes = product[:, 0:128] + product[:, 128:256]
+            ssq_out[rows, :] = lanes if half == 0 else ssq_out[rows, :] + lanes
+        gstage[:, cols] = partial
+
+    compared(0, moved)
+    compared(1, moved_last)
     to_rows(ssq_out, stage.at[2])
     inner = exchange(2)
-    gstage[...] = partial
     gained = [net.copy(gstage, gains.at[p.s], d) for d in students]
     net.sent(hop1)
     to_columns(exchanged(2, inner) / DS, sq_out)
@@ -570,12 +673,18 @@
             V((1024, 1024), BF),
             V((1024, 512), BF),
             V((1024, 1024), BF),
+            V((1024, 1024), BF),
             V((2, 512, 512), BF),
+            V((2, 512, 128), BF),
+            V((4, 2, 512, 128), BF),
             V((2, 512, 256), BF),
-            V((2, 512, 512), BF),
-            V((2, 2, 512, 512), BF),
-            V((2, 2, 1024, 512), BF),
-            V((1024, 512), BF),
+            V((4, 2, 512, 256), BF),
+            V((4, 1024, 256), BF),
+            V((2, 2, 512, 256), BF),
+            V((2, 2, 1024, 256), BF),
+            V((2, 512, 256), BF),
+            V((2, 1024, 256), BF),
+            V((1024, 256), BF),
             V((1024, 512), BF),
             V((1024, 128), F32),
             V((1024, 512), F32),
@@ -587,7 +696,6 @@
             V((7, 128, 512), BF),
             V((16, 8, 128), jnp.int32),
             V((4, 128, 128), F32),
-            V((1024, 128), F32),
             V((1024, 128), F32),
             V((1024, 128), F32),
             V((3, 8, 128), F32),

time: 260 us -> 230 us (0.88)
  Pallas kernels: 254 us -> 223 us
    pallas_call x1, Pallas kernels: 254 us -> 223 us  [step(): pl.pallas_call(step_kernel, out_shape=(jax.ShapeDtypeStruct((128, 512), F...]
where the time goes in v3:
time: 230 us; the launch traced here: 229 us
  Pallas kernels  223 us (97%)
  local copies, waits for them, and re-layouts  2.92 us (1%)
  other arithmetic  2.53 us (1%)
    pallas_call x1, Pallas kernels, step(): pl.pallas_call(step_kernel, out_shape=(jax.ShapeDtypeStruct((128, 512), F...  223 us

profile of v3, /device:TPU:1, one launch (start us, length us, event | category | flops | bytes accessed | tf_op | source)
XLA Modules:
  0.0 229.4 jit_solution(6043702071977959788)
XLA Ops:
  0.6 1.3 reshape.32
  1.9 1.3 reshape.30
  3.2 223.3 %step.1 = (f32[128,512]{1,0:T(8,128)}, f32[1,512]{1,0:T(1,128)}) custom-call(bf16[1024,1024]{1,0:T(8,128)(2,1)} %tin.1, bf16[1024,512]{1,0:T(8,128)(2,1)} %tattn.1, bf16[256,1024]{1,0:T(8,128)(2,1)} %tw.1, f32[1,1024]{1,0:T(1,128)} %bitcast.6, bf16[1024,256]{1,0:T(8,128)(2,1)} %proj.1, bf16[1024,512]{1,0:T(8,128)(2,1)} %sin.1, bf16[1024,256]{1,0:T(8,128)(2,1)} %sattn.1, ...), custom_call_target="tpu_custom_call" | custom-call | tf_op jit(solution)/shard_map/step/pallas_call | solution.py:659
  226.5 1.7 copy.15
  228.1 1.2 copy.16

commit v4 on v3

--- a/solution.py
+++ b/solution.py
@@ -104,12 +104,12 @@
 
 
 def step_kernel(
-    tin, tattn, tw, tgain, proj, sin, sattn, su, sgain, tokens, order,
+    tin, tattn, tw, tgain_in, proj, sin, sattn, su, sgain_in, tokens, order_in,
     weight_out, gain_out,
     bufA, bufC, bufW, bufP, bufU, tinv, sinv, hid,
     pick, tmpA, tmpC, tmpD, tmpE, tmpZ, rz, r1, r2, b1, b2, r3, zs,
     sq_out, sres_out, ssq_out, target, frecv, gn, sibr, grecv, tok, rowbuf,
-    scol, lcol, stage, exch, gstage, gains,
+    tgain, sgain, order, scol, lcol, stage, exch, gstage, gains,
     send, recv, local,
 ):
     p = Place()
@@ -233,7 +233,8 @@
     ahop1 = t_hop1(A)
     for n, arr in (("W", W), ("Q", Q)):
         sowns[n] = s_own(arr)
-        ssides[n] = s_side(arr)
+        if n == "W":
+            ssides[n] = s_side(arr)
         shared.append(net.copy(arr[0], arr[1].at[p.s], sib))
     bring(tattn, bufA.at[p.t])
     bring(tw, bufW.at[p.s])
@@ -245,26 +246,30 @@
     down_ = t_own(D)
     told = [net.copy(tokens, tok.at[p.s], d) for d in students]
     bring(tokens, tok.at[p.s])
+    bring(tgain_in, tgain)
+    bring(sgain_in, sgain)
+    bring(order_in, order)
     sowns["U"] = s_own(U)
-    ssides["U"] = s_side(U)
     shared.append(net.copy(U[0], U[1].at[p.s], sib))
     S = (("W", W), ("Q", Q), ("U", U))
     sfwd, sfwd2, sparts = {}, {}, {}
 
     ahop2 = t_hop2(A, ahop1)
     dhop1, dhop2 = {}, {}
+    ssides["Q"] = s_side(Q)
     dhop1[0] = d_hop1(0)
+    ssides["U"] = s_side(U)
     for n, arr in S[:2]:
         sfwd[n] = s_forward(arr, *sowns[n], False)
     afwd = t_forward(A, *aown, 0)
     sparts["W"] = s_partner(W, ssides["W"])
-    dhop2[0] = d_hop2(0, dhop1[0])
-    sparts["Q"] = s_partner(Q, ssides["Q"])
+    dfwd = t_forward(D, *down_, 0)
     apart = t_partner(A, ahop2)
-    dfwd = t_forward(D, *down_, 0)
     got(down_[0][1], down_[1][0])
     dhop1[-1] = d_hop1(-1)
     dhop1[1] = d_hop1(1)
+    dhop2[0] = d_hop2(0, dhop1[0])
+    sparts["Q"] = s_partner(Q, ssides["Q"])
     for n, arr in S[:2]:
         got(sowns[n][0][1], sowns[n][1][0])
         shared.append(share(arr, sp))
@@ -345,7 +350,7 @@
             acc = acc + jnp.dot(bufA[t, rows, :], w, preferred_element_type=F32)
         square = acc * acc
         sq_out[rows, :] += square[:, 0:128] + square[:, 128:256] + square[:, 256:384] + square[:, 384:512]
-        hid[rows, cols] = (acc * tgain[:, cols]).astype(BF)
+        hid[rows, cols] = (acc * tgain[cols].astype(F32).reshape(1, 512)).astype(BF)
         return carry
 
     lax.fori_loop(0, 2, first, 0)
@@ -584,7 +589,7 @@
 
     def compared(half, copies):
         cols = columns(half)
-        gain_values = sgain[:, cols]
+        gain_values = sgain[cols].astype(F32).reshape(1, 256)
         partial = jnp.zeros((1, 256), F32)
         for m in (0, *range(4, 16), 1, 2, 3):
             if m:
@@ -662,7 +667,7 @@
             jax.ShapeDtypeStruct((128, 512), F32),
             jax.ShapeDtypeStruct((1, 512), F32),
         ),
-        in_specs=[anywhere] * 3 + [vmem] + [anywhere] * 4 + [vmem, anywhere, vmem],
+        in_specs=[anywhere] * 11,
         out_specs=(vmem, vmem),
         scratch_shapes=[
             V((8, 1024, 512), BF),
@@ -696,6 +701,9 @@
             V((7, 128, 512), BF),
             V((16, 8, 128), jnp.int32),
             V((4, 128, 128), F32),
+            V((1024,), BF),
+            V((512,), BF),
+            V((128, 128), jnp.int32),
             V((1024, 128), F32),
             V((1024, 128), F32),
             V((3, 8, 128), F32),
@@ -711,8 +719,8 @@
         ),
         name="step",
     )(
-        tin, tattn, tw, tgain.astype(F32).reshape(1, -1), proj, sin, sattn, su,
-        sgain.astype(F32).reshape(1, -1), token_ids.reshape(8, 128), row_order.reshape(128, 128),
+        tin, tattn, tw, tgain, proj, sin, sattn, su,
+        sgain, token_ids.reshape(8, 128), row_order.reshape(128, 128),
     )
     return weight, gain.reshape(512)
 

time: 230 us -> 210 us (0.913)
  Pallas kernels: 223 us -> 206 us
  other arithmetic: 2.53 us -> 0 us
    pallas_call x1, Pallas kernels: 223 us -> 206 us  [step(): pl.pallas_call(step_kernel, out_shape=(jax.ShapeDtypeStruct((128, 512), F...]
    reshape x2 -> x0, other arithmetic: 2.53 us -> none  [the longest x1 1.27 us: step(): tgain.astype(F32).reshape(1, -1)]
where the time goes in v4:
time: 210 us
  Pallas kernels  206 us (98%)
  local copies, waits for them, and re-layouts  2.92 us (1%)
    pallas_call x1, Pallas kernels, step(): pl.pallas_call(step_kernel, out_shape=(jax.ShapeDtypeStruct((128, 512), F...  206 us

profile of v4, /device:TPU:1, one launch (start us, length us, event | category | flops | bytes accessed | tf_op | source)
XLA Modules:
  0.0 209.9 jit_solution(3351576673885975041)
XLA Ops:
  0.6 206.3 %step.1 = (f32[128,512]{1,0:T(8,128)}, f32[1,512]{1,0:T(1,128)}) custom-call(bf16[1024,1024]{1,0:T(8,128)(2,1)} %tin.1, bf16[1024,512]{1,0:T(8,128)(2,1)} %tattn.1, bf16[256,1024]{1,0:T(8,128)(2,1)} %tw.1, bf16[1024]{0:T(1024)(128)(2,1)} %tgain_in.1, bf16[1024,256]{1,0:T(8,128)(2,1)} %proj.1, bf16[1024,512]{1,0:T(8,128)(2,1)} %sin.1, ...), custom_call_target="tpu_custom_call" | custom-call | tf_op jit(solution)/shard_map/step/pallas_call | solution.py:664
  207.0 1.7 copy.15
  208.6 1.2 copy.16

commit v5 on v4

--- a/solution.py
+++ b/solution.py
@@ -464,7 +464,6 @@
     z_first(-1)
     added_far = added(True, 0, open_far, r1.at[0], r2.at[0])
     z_on(1)
-    z_first(0)
     project(block(False, 1), 0)
     up_near = plain_up(False, 0, r2.at[1])
     project(block(False, -1), 0)
@@ -474,6 +473,11 @@
     k_far, k_near = block(True, 0), block(False, 0)
     project(k_far, 0)
     project(k_near, 0)
+    z_on(-1)
+    z_first(0)
+    z_add(2)
+    opened = open_to(block(False, 2), 1, b1)
+    added_near = added(False, 0, open_near, r1.at[1], r2.at[1])
     got(cown[0][1], cown[1][0], *cfwd, cpart[0][1], cpart[1][0], *cfwd2)
     got(*dhop2[0], *dhop2[1], *dhop2[-1], *dhop2[2])
     got(*sfwd2["U"])
@@ -506,10 +510,6 @@
             bufW[core * 4 + div(t, 2), at, rows] = turned.astype(BF)
         return carry
 
-    z_on(-1)
-    z_add(2)
-    opened = open_to(block(False, 2), 1, b1)
-    added_near = added(False, 0, open_near, r1.at[1], r2.at[1])
     lax.fori_loop(0, 16, turn, 0)
 
     def three(k, half, src, i):
@@ -626,23 +626,31 @@
     def product(core, i):
         return jnp.dot(bufW[core * 4 + i], zs[...], preferred_element_type=F32)
 
-    halves = []
-    for i in range(4):
-        sinv[i * 256 : i * 256 + 256, :] = product(1 - p.core, i).astype(BF)
-        part = pl.ds(i * 256, 256)
-        halves.append(net.copy(sinv.at[part, :], sibr.at[part, :], sib))
-    for i in range(4):
-        own_part = product(p.core, i)
-        got(halves[i])
-        total = own_part + sibr[i * 256 : i * 256 + 256, :].astype(F32)
-        tinv[i * 256 : i * 256 + 256, 512:1024] = total.astype(BF)
+    halves = {}
+    for j in (2, 3, 1, 0):
+        i = rem(div(p.s, 4) + j, 4)
+        part = pl.ds(pl.multiple_of(i * 256, 256), 256)
+        sinv[part, :] = product(1 - p.core, i).astype(BF)
+        halves[j] = net.copy(sinv.at[part, :], sibr.at[part, :], sib)
     chip = div(p.s, 2)
     parts = []
-    for m in range(1, 8):
-        q = rem(chip + m, 8)
-        rows = pl.ds(pl.multiple_of(q * 128, 128), 128)
-        to = {"teacher": p.t, "student": q * 2 + p.core}
-        parts.append(net.copy(tinv.at[rows, right], grecv.at[m - 1], to))
+    for j in (2, 3, 1, 0):
+        i = rem(div(chip, 2) + j, 4)
+        own_part = product(p.core, i)
+        rows = pl.ds(pl.multiple_of(i * 256, 256), 256)
+        got(halves[j])
+        total = own_part + sibr[rows, :].astype(F32)
+        tinv[rows, 512:1024] = total.astype(BF)
+        for n in range(2):
+            if j == 0 and n == 1:
+                continue
+            if j == 0:
+                q = i * 2 + 1 - rem(chip, 2)
+            else:
+                q = i * 2 + rem(chip + n, 2)
+            sub_rows = pl.ds(pl.multiple_of(q * 128, 128), 128)
+            to = {"teacher": p.t, "student": q * 2 + p.core}
+            parts.append(net.copy(tinv.at[sub_rows, right], grecv.at[len(parts)], to))
     gains[p.s] = gstage[...]
     got(*gained)
     total_gain = gains[0]

time: 210 us -> 208 us (level)
  Pallas kernels: 206 us -> 203 us
    pallas_call x1, Pallas kernels: 206 us -> 203 us  [step(): pl.pallas_call(step_kernel, out_shape=(jax.ShapeDtypeStruct((128, 512), F...]
where the time goes in v5:
time: 208 us; the launch traced here: 207 us
  Pallas kernels  203 us (98%)
  local copies, waits for them, and re-layouts  2.92 us (1%)
    pallas_call x1, Pallas kernels, step(): pl.pallas_call(step_kernel, out_shape=(jax.ShapeDtypeStruct((128, 512), F...  203 us

profile of v5, /device:TPU:1, one launch (start us, length us, event | category | flops | bytes accessed | tf_op | source)
XLA Modules:
  0.0 207.0 jit_solution(4430823037084707010)
XLA Ops:
  0.6 203.5 %step.1 = (f32[128,512]{1,0:T(8,128)}, f32[1,512]{1,0:T(1,128)}) custom-call(bf16[1024,1024]{1,0:T(8,128)(2,1)} %tin.1, bf16[1024,512]{1,0:T(8,128)(2,1)} %tattn.1, bf16[256,1024]{1,0:T(8,128)(2,1)} %tw.1, bf16[1024]{0:T(1024)(128)(2,1)} %tgain_in.1, bf16[1024,256]{1,0:T(8,128)(2,1)} %proj.1, bf16[1024,512]{1,0:T(8,128)(2,1)} %sin.1, ...), custom_call_target="tpu_custom_call" | custom-call | tf_op jit(solution)/shard_map/step/pallas_call | solution.py:672
  204.1 1.7 copy.15
  205.8 1.2 copy.16

commit v6 on v5

--- a/solution.py
+++ b/solution.py
@@ -105,11 +105,11 @@
 
 def step_kernel(
     tin, tattn, tw, tgain_in, proj, sin, sattn, su, sgain_in, tokens, order_in,
-    weight_out, gain_out,
+    grecv, gains,
     bufA, bufC, bufW, bufP, bufU, tinv, sinv, hid,
     pick, tmpA, tmpC, tmpD, tmpE, tmpZ, rz, r1, r2, b1, b2, r3, zs,
-    sq_out, sres_out, ssq_out, target, frecv, gn, sibr, grecv, tok, rowbuf,
-    tgain, sgain, order, scol, lcol, stage, exch, gstage, gains,
+    sq_out, sres_out, ssq_out, target, frecv, gn, sibr, tok, rowbuf,
+    tgain, sgain, order, scol, lcol, stage, exch, gstage,
     send, recv, local,
 ):
     p = Place()
@@ -517,6 +517,8 @@
         own_part = bufA[k, at, columns(half)].astype(F32)
         return at, own_part + src[0, at, :].astype(F32) + src[1, at, :].astype(F32)
 
+    z_add(1)
+    up_last = plain_up(False, 1, b2)
     got(up_far, down_far, *added_far)
 
     def far_sum(i, carry):
@@ -529,8 +531,6 @@
         net.copy(zs.at[lo, columns(0)], tmpE.at[0], p.dev(dz=1)),
         net.copy(zs.at[hi, columns(0)], tmpE.at[1], p.dev(dz=-1)),
     )
-    z_add(1)
-    up_last = plain_up(False, 1, b2)
     z_on(0)
     to_rows(sq_out, stage.at[0])
     tsums = exchange(0)
@@ -651,32 +651,27 @@
             sub_rows = pl.ds(pl.multiple_of(q * 128, 128), 128)
             to = {"teacher": p.t, "student": q * 2 + p.core}
             parts.append(net.copy(tinv.at[sub_rows, right], grecv.at[len(parts)], to))
-    gains[p.s] = gstage[...]
-    got(*gained)
-    total_gain = gains[0]
-    for b in range(1, 16):
-        total_gain = total_gain + gains[b]
-    gain_out[...] = total_gain
-    total = tinv[pl.ds(pl.multiple_of(chip * 128, 128), 128), 512:1024].astype(F32)
-    for m in range(7):
-        got(parts[m])
-        total = total + grecv[m].astype(F32)
-    weight_out[...] = total
+    last = [
+        bring(gstage, gains.at[p.s]),
+        bring(tinv.at[pl.ds(pl.multiple_of(chip * 128, 128), 128), right], grecv.at[7]),
+    ]
+    for c in last:
+        c.wait()
+    got(*gained, *parts)
     net.finish()
 
 
 def step(tin, tattn, tw, tgain, proj, sin, sattn, su, sgain, token_ids, row_order):
     anywhere = pl.BlockSpec(memory_space=pl.ANY)
-    vmem = pl.BlockSpec(memory_space=pltpu.VMEM)
     V = pltpu.VMEM
-    weight, gain = pl.pallas_call(
+    parts, gains = pl.pallas_call(
         step_kernel,
         out_shape=(
-            jax.ShapeDtypeStruct((128, 512), F32),
-            jax.ShapeDtypeStruct((1, 512), F32),
+            jax.ShapeDtypeStruct((8, 128, 512), BF),
+            jax.ShapeDtypeStruct((16, 1, 512), F32),
         ),
         in_specs=[anywhere] * 11,
-        out_specs=(vmem, vmem),
+        out_specs=(anywhere, anywhere),
         scratch_shapes=[
             V((8, 1024, 512), BF),
             V((8, 1024, 256), BF),
@@ -706,7 +701,6 @@
             V((16, 64, 512), BF),
             V((1024, 512), F32),
             V((1024, 512), BF),
-            V((7, 128, 512), BF),
             V((16, 8, 128), jnp.int32),
             V((4, 128, 128), F32),
             V((1024,), BF),
@@ -717,7 +711,6 @@
             V((3, 8, 128), F32),
             V((3, 8, 8, 128), F32),
             V((1, 512), F32),
-            V((16, 1, 512), F32),
             pltpu.SemaphoreType.DMA((SLOTS,)),
             pltpu.SemaphoreType.DMA((SLOTS,)),
             pltpu.SemaphoreType.DMA((16,)),
@@ -730,7 +723,7 @@
         tin, tattn, tw, tgain, proj, sin, sattn, su,
         sgain, token_ids.reshape(8, 128), row_order.reshape(128, 128),
     )
-    return weight, gain.reshape(512)
+    return jnp.sum(parts.astype(F32), axis=0), jnp.sum(gains, axis=(0, 1))
 
 
 def solution(mesh):

time: 208 us -> 208 us (level)
  other arithmetic: 0 us -> 3.46 us
  local copies, waits for them, and re-layouts: 2.92 us -> 0 us
    reduce_sum x0 -> x2, other arithmetic: none -> 3.46 us  [step(): return (jnp.sum(parts.astype(F32), axis=0), jnp.sum(gains, axis=(0, 1)))]
    unnamed x2 -> x0, local copies, waits for them, and re-layouts: 2.92 us -> none
where the time goes in v6:
time: 208 us; the launch traced here: 207 us
  Pallas kernels  203 us (98%)
  other arithmetic  3.46 us (2%)
    pallas_call x1, Pallas kernels, step(): pl.pallas_call(step_kernel, out_shape=(jax.ShapeDtypeStruct((8, 128, 512)...  203 us

profile of v6, /device:TPU:1, one launch (start us, length us, event | category | flops | bytes accessed | tf_op | source)
XLA Modules:
  0.0 207.0 jit_solution(12994597445606054113)
XLA Ops:
  0.6 202.9 %step.1 = (bf16[8,128,512]{2,1,0:T(8,128)(2,1)}, f32[16,1,512]{2,1,0:T(1,128)}) custom-call(bf16[1024,1024]{1,0:T(8,128)(2,1)} %tin.1, bf16[1024,512]{1,0:T(8,128)(2,1)} %tattn.1, bf16[256,1024]{1,0:T(8,128)(2,1)} %tw.1, bf16[1024]{0:T(1024)(128)(2,1)} %tgain_in.1, bf16[1024,256]{1,0:T(8,128)(2,1)} %proj.1, bf16[1024,512]{1,0:T(8,128)(2,1)} %sin.1, ...), custom_call_target="tpu_custom_call" | custom-call | tf_op jit(solution)/shard_map/step/pallas_call | solution.py:667
  203.5 2.1 %convert_reduce_fusion = f32[128,512]{1,0:T(8,128)} fusion(bf16[8,128,512]{2,1,0:T(8,128)(2,1)} %get-tuple-element.4), kind=kLoop, calls=%fused_computation | loop fusion | flops 983040 | bytes 1310720 | tf_op jit(solution)/shard_map/reduce_sum | solution.py:726
  205.6 1.4 reduce_sum.19
